TPU v7x, 32 devices: a whole 2x2x4 slice. The times are simulated.
32 devices in a mesh: freq: 8 (over y, x, core), feed: 4 (over z).
Axes of the slice: x: 2, y: 2, z: 4, core: 2. Of those that a mesh axis runs over, the one named last changes fastest.
Arguments:
- voltages: int32 [32, 2048, 2, 768], P(None, ('feed', 'freq')), may hold values from -127 to 127
- gains: float32 [2, 32, 2048], P(None, None, ('feed', 'freq')), may hold values from -0.06 to 0.06
Outputs:
- visibilities: float32 [32, 2, 2048, 2048], P('freq', None, 'feed')
All inputs are finite; a program needn't handle non-finite values.
Results may differ from a plain program's by a relative error of at most 0.0031.
Values may be sent and summed in bfloat16 or wider, within the bound.
No kernel may reach another device: no remote copies, remote signals or barrier semaphores. Data moves between devices by JAX's collectives and lax.ppermute only.
A program may use at most 192 MiB of HBM per device.

v0:
```python
import jax
import jax.numpy as jnp
from jax import lax
from jax.sharding import PartitionSpec as P


def stack_rows(own_rows, samples):
    real_part = own_rows[..., :samples]
    imag_part = own_rows[..., samples:]
    swapped = jnp.concatenate([imag_part, -real_part], axis=-1)
    return jnp.stack([own_rows, swapped], axis=1)


def correlate(stacked, columns, samples):
    product = jnp.einsum("cqrk,cfk->cqrf", stacked, columns, preferred_element_type=jnp.float32)
    return product * (1.0 / samples)


def per_device(voltages, gains):
    channels = voltages.shape[0]
    local_feeds = voltages.shape[1]
    samples = voltages.shape[3]
    freq_count = lax.axis_size("freq")
    owned = channels // freq_count
    volt_real = voltages[:, :, 0, :].astype(jnp.float32)
    volt_imag = voltages[:, :, 1, :].astype(jnp.float32)
    gain_real = gains[0][:, :, None]
    gain_imag = gains[1][:, :, None]
    eq_real = gain_real * volt_real - gain_imag * volt_imag
    eq_imag = gain_real * volt_imag + gain_imag * volt_real
    equalized = jnp.stack([eq_real, eq_imag], axis=2).astype(jnp.bfloat16)
    blocks = equalized.reshape(freq_count, owned, local_feeds, 2 * samples)
    arrived = lax.all_to_all(blocks, "freq", split_axis=0, concat_axis=2, tiled=True)
    own_rows = arrived[0]
    stacked = stack_rows(own_rows, samples)
    return correlate(stacked, lax.all_gather(own_rows, "feed", axis=1, tiled=True), samples)


def solution(mesh):
    in_specs = (P(None, ("feed", "freq"), None, None), P(None, None, ("feed", "freq")))
    out_specs = P("freq", None, "feed", None)
    return jax.shard_map(
        per_device, mesh=mesh, in_specs=in_specs, out_specs=out_specs, check_vma=False
    )
```

profile of v0, /device:TPU:0, one launch (start us, length us, event | category | flops | bytes accessed | tf_op | source)
XLA Modules:
  0.0 606.3 jit_solution(17884581884118223520)
XLA Ops:
  6.5 0.0 all-gather.2.cloned.1.call-start
  6.5 0.7 slice_bitcast_fusion.1
  7.3 22.8 %subtract_convert_fusion = (bf16[32,64,1,768]{3,2,1,0:T(2,128)(2,1)S(1)}, bf16[32,64,1,768]{3,2,1,0:T(2,128)(2,1)S(1)}) fusion(s32[32,64,2,768]{3,2,1,0:T(2,128)} %param.2, f32[32,64]{1,0:T(8,128)S(1)} %get-tuple-element.10, f32[32,64]{1,0:T(8,128)S(1)} %get-tuple-element.9), kind=kLoop, calls=%fused_computation.8 | loop fusion | flops 15728640 | bytes 18890752 | tf_op jit(solution)/shard_map/convert
  30.0 15.4 %pad_maximum_fusion.1 = bf16[32,64,2,768]{3,2,1,0:T(2,128)(2,1)} fusion(bf16[32,64,1,768]{3,2,1,0:T(2,128)(2,1)S(1)} %get-tuple-element.6, bf16[32,64,1,768]{3,2,1,0:T(2,128)(2,1)S(1)} %get-tuple-element.5), kind=kLoop, calls=%fused_computation.5 | loop fusion | flops 12582912 | bytes 12582912 | tf_op jit(solution)/shard_map/stack | solution.py:31
  45.4 14.4 %convert_element_type.17 = bf16[8,4,64,1536]{3,2,1,0:T(8,128)(2,1)} reshape(bf16[32,64,2,768]{3,2,1,0:T(2,128)(2,1)} %pad_maximum_fusion.1) | data formatting | bytes 12582912 | tf_op jit(solution)/shard_map/convert_element_type | solution.py:31
  59.8 76.7 %all_to_all.15 = bf16[8,4,64,1536]{3,2,1,0:T(8,128)(2,1)S(1)} all-to-all(bf16[8,4,64,1536]{3,2,1,0:T(8,128)(2,1)} %convert_element_type.17), channel_id=1, replica_groups=mesh['freq'=8,'feed'=4] {'freq'}, dimensions={0} | all-to-all | bytes 12582912 | tf_op jit(solution)/shard_map/all_to_all | solution.py:33
  136.5 3.4 copy.5
  139.9 0.0 all-gather.2.cloned.1.call-update
  140.0 3.3 fusion.6
  143.2 3.3 maximum_bitcast_fusion
  146.5 417.1 %all-gather.2.cloned.1.call-done = bf16[4,2048,1536]{2,1,0:T(8,128)(2,1)} async-done(((bf16[4,512,1536]{2,1,0:T(8,128)(2,1)}), bf16[4,2048,1536]{2,1,0:T(8,128)(2,1)}) %all-gather.2.cloned.1.call-update) | async-done | bytes 25165840 | tf_op jit(solution)/shard_map/all_gather | solution.py:36
  563.6 35.8 %fusion.2 = f32[4,2,512,2048]{3,2,1,0:T(8,128)} fusion(bf16[4,2048,1536]{2,1,0:T(8,128)(2,1)} %all-gather.2.cloned.1.call-done, bf16[4,1,512,1536]{3,2,0,1:T(8,128)(2,1)} %maximum_bitcast_fusion, bf16[4,1,512,1536]{3,2,0,1:T(8,128)(2,1)} %bitcast.20), kind=kOutput, calls=%fused_computation.2 | convolution fusion | flops 25784483840 | bytes 71303168 | tf_op jit(solution)/shard_map/cqrk,cfk->cqrf/dot_general | solution.py:15
Async XLA Ops:
  6.5 557.1 %all-gather.2.cloned.1.call-start = ((), (), s32[]{:S(2)}) async-start(), calls=%async_computation.1 | async-start | bytes 31457280 | tf_op jit(solution)/shard_map/all_gather | solution.py:36
Sparse Core Ops, SparseCore 0:
  140.1 423.5 all-gather.1
where the time goes:
time: 607 us; the launch traced here: 606 us
  waiting for transfers between devices  417 us (69%)
  blocking collectives  76.7 us (13%)
  other arithmetic  44.7 us (7%)
  matrix products  35.8 us (6%)
  local copies, waits for them, and re-layouts  18.5 us (3%)
  between operations  13.4 us (2%)
    all_gather x1, waiting for transfers between devices, per_device(): lax.all_gather(own_rows, 'feed', axis=1, tiled=True)  417 us
    all_to_all x1, blocking collectives, per_device(): lax.all_to_all(blocks, 'freq', split_axis=0, concat_axis=2, tiled=True)  76.7 us
    dot_general x1, matrix products, correlate(): jnp.einsum('cqrk,cfk->cqrf', stacked, columns, preferred_element_type=jnp...  35.8 us
    another operation x1, other arithmetic  22.8 us
    another operation x1, other arithmetic, per_device(): equalized = jnp.stack([eq_real, eq_imag], axis=2).astype(jnp.bfloat16)  15.4 us
    convert_element_type x1, local copies, waits for them, and re-layouts, per_device(): equalized = jnp.stack([eq_real, eq_imag], axis=2).astype(jnp.bfloat16)  14.4 us
  transfers between devices with their start and end apart: 1, of which 1 were waited for; matrix products, arithmetic and copies ran while one was open for 1% of the time, Pallas kernels for 0%

commit v1 on v0

v1 whole, which is shorter than its diff:
```python
import functools

import jax
import jax.numpy as jnp
from jax import lax
from jax.experimental import pallas as pl
from jax.experimental.pallas import tpu as pltpu
from jax.sharding import PartitionSpec as P

CONTRACT_LAST = (((1,), (1,)), ((), ()))
INWARD = ((0, 1), (3, 2))
MIDDLE = ((1, 2), (2, 1))
OUTWARD = ((1, 0), (2, 3))


def equalize_kernel(volt_ref, gain_ref, out_ref):
    samples = volt_ref.shape[-1]
    gain_real = gain_ref[0, :, 0:1]
    gain_imag = gain_ref[0, :, 1:2]
    volt_real = volt_ref[0, :, 0, :].astype(jnp.float32)
    volt_imag = volt_ref[0, :, 1, :].astype(jnp.float32)
    out_ref[0, :, :samples] = (gain_real * volt_real - gain_imag * volt_imag).astype(jnp.bfloat16)
    out_ref[0, :, samples:] = (gain_real * volt_imag + gain_imag * volt_real).astype(jnp.bfloat16)


def equalize(voltages, gains, chunk, freq_count):
    channels, feeds, _, samples = voltages.shape
    owned = channels // freq_count
    return pl.pallas_call(
        equalize_kernel,
        grid=(freq_count,),
        in_specs=[
            pl.BlockSpec((1, feeds, 2, samples), lambda f: (f * owned + chunk, 0, 0, 0)),
            pl.BlockSpec((1, feeds, 2), lambda f: (f * owned + chunk, 0, 0)),
        ],
        out_specs=pl.BlockSpec((1, feeds, 2 * samples), lambda f: (f, 0, 0)),
        out_shape=jax.ShapeDtypeStruct((freq_count, feeds, 2 * samples), jnp.bfloat16),
        cost_estimate=pl.CostEstimate(
            flops=6 * freq_count * feeds * samples * 2,
            bytes_accessed=freq_count * feeds * samples * 12,
            transcendentals=0,
        ),
        name="equalize",
    )(voltages, gains)


def visibility(left, right, samples):
    turned = jnp.concatenate([-right[:, samples:], right[:, :samples]], axis=1)
    real_part = lax.dot_general(left, right, CONTRACT_LAST, preferred_element_type=jnp.float32)
    imag_part = lax.dot_general(left, turned, CONTRACT_LAST, preferred_element_type=jnp.float32)
    return real_part * (1.0 / samples), imag_part * (1.0 / samples)


def own_kernel(place_ref, own_ref, other_ref, *refs):
    out_ref = refs[-1]
    samples = own_ref.shape[1] // 2
    real_part, imag_part = visibility(own_ref[...], other_ref[...], samples)
    out_ref[0, 0] = real_part
    out_ref[0, 1] = imag_part


def own_block(out, out_shape, chunk, place, own, other, name):
    rows, depth = own.shape
    half = rows // 2
    in_specs = [
        pl.BlockSpec((rows, depth), lambda j, p: (0, 0)),
        pl.BlockSpec((half, depth), lambda j, p: (j, 0)),
    ]
    operands = [own, other]
    aliases = {}
    if out is not None:
        in_specs.append(pl.BlockSpec(memory_space=pl.ANY))
        operands.append(out)
        aliases = {3: 0}
    return pl.pallas_call(
        own_kernel,
        grid_spec=pltpu.PrefetchScalarGridSpec(
            num_scalar_prefetch=1,
            grid=(2,),
            in_specs=in_specs,
            out_specs=pl.BlockSpec((1, 2, rows, half), lambda j, p: (chunk, 0, 0, p[0] * 2 + j)),
        ),
        out_shape=out_shape,
        input_output_aliases=aliases,
        cost_estimate=pl.CostEstimate(
            flops=4 * rows * rows * depth, bytes_accessed=4 * rows * depth + 8 * rows * rows, transcendentals=0
        ),
        name=name,
    )(place, *operands)


def pair_kernel(place_ref, own_ref, end_ref, other_ref, rest_other_ref, _, out_ref, rest_ref):
    samples = own_ref.shape[1] // 2

    @pl.when(place_ref[1] == 1)
    def _():
        real_part, imag_part = visibility(own_ref[...], other_ref[...], samples)
        out_ref[0, 0] = real_part
        out_ref[0, 1] = imag_part
        real_part, imag_part = visibility(end_ref[...], rest_other_ref[...], samples)
        rest_ref[0] = real_part.astype(jnp.bfloat16)
        rest_ref[1] = imag_part.astype(jnp.bfloat16)


def pair_block(out, chunk, place, own, end, other, rest_other, name):
    rows, depth = own.shape
    half = rows // 2
    whole = pl.BlockSpec((rows, depth), lambda j, p: (0, 0))
    tile = pl.BlockSpec((half, depth), lambda j, p: (j, 0))
    return pl.pallas_call(
        pair_kernel,
        grid_spec=pltpu.PrefetchScalarGridSpec(
            num_scalar_prefetch=1,
            grid=(2,),
            in_specs=[whole, whole, tile, tile, pl.BlockSpec(memory_space=pl.ANY)],
            out_specs=[
                pl.BlockSpec((1, 2, rows, half), lambda j, p: (chunk, 0, 0, p[0] * 2 + j)),
                pl.BlockSpec((2, rows, half), lambda j, p: (0, 0, j)),
            ],
        ),
        out_shape=[
            jax.ShapeDtypeStruct(out.shape, out.dtype),
            jax.ShapeDtypeStruct((2, rows, rows), jnp.bfloat16),
        ],
        input_output_aliases={5: 0},
        cost_estimate=pl.CostEstimate(
            flops=8 * rows * rows * depth, bytes_accessed=8 * rows * depth + 12 * rows * rows, transcendentals=0
        ),
        name=name,
    )(place, own, end, other, rest_other, out)


def settle_kernel(chunks, rows, place_ref, *refs):
    count = len(chunks)
    rest_refs = refs[:count]
    out_ref, buf, sems = refs[count + 1:]

    @pl.when(place_ref[0] == 0)
    def _():
        copies = []
        for b in range(count):
            for part in range(2):
                buf[b, part] = rest_refs[b][part].astype(jnp.float32)
                column = pl.multiple_of(place_ref[1 + b] * rows, rows)
                copy = pltpu.make_async_copy(
                    buf.at[b, part],
                    out_ref.at[chunks[b], part, :, pl.ds(column, rows)],
                    sems.at[b, part],
                )
                copy.start()
                copies.append(copy)
        for copy in copies:
            copy.wait()


def settle(out, is_mid, items):
    chunks = [chunk for chunk, _, _ in items]
    place = jnp.stack([is_mid] + [column for _, column, _ in items]).astype(jnp.int32)
    rests = [made for _, _, made in items]
    count = len(items)
    rows = rests[0].shape[1]
    return pl.pallas_call(
        functools.partial(settle_kernel, chunks, rows),
        grid_spec=pltpu.PrefetchScalarGridSpec(
            num_scalar_prefetch=1,
            grid=(1,),
            in_specs=[pl.BlockSpec((2, rows, rows), lambda i, p: (0, 0, 0))] * count
            + [pl.BlockSpec(memory_space=pl.ANY)],
            out_specs=pl.BlockSpec(memory_space=pl.ANY),
            scratch_shapes=[
                pltpu.VMEM((count, 2, rows, rows), jnp.float32),
                pltpu.SemaphoreType.DMA((count, 2)),
            ],
        ),
        out_shape=jax.ShapeDtypeStruct(out.shape, out.dtype),
        input_output_aliases={1 + count: 0},
        cost_estimate=pl.CostEstimate(
            flops=count * 2 * rows * rows, bytes_accessed=12 * count * rows * rows, transcendentals=0
        ),
        name="settle",
    )(place, *rests, out)


def per_device_line(voltages, gains):
    channels, local_feeds, _, samples = voltages.shape
    freq_count = lax.axis_size("freq")
    feed_count = lax.axis_size("feed")
    owned = channels // freq_count
    rows = local_feeds * freq_count
    z = lax.axis_index("feed")
    is_mid = ((z == 1) | (z == 2)).astype(jnp.int32)
    low = z < 2
    near_end = jnp.where(low, 0, 3)
    near_mid = jnp.where(low, 1, 2)
    far_mid = 3 - near_mid
    far_end = 3 - near_end
    place_own = jnp.stack([z, is_mid]).astype(jnp.int32)
    place_near = jnp.stack([jnp.where(is_mid == 1, near_end, near_mid), is_mid]).astype(jnp.int32)
    place_mid = jnp.stack([far_mid, is_mid]).astype(jnp.int32)
    place_far = jnp.stack([far_end, is_mid]).astype(jnp.int32)
    gain_cols = jnp.transpose(gains, (1, 2, 0))
    out_shape = jax.ShapeDtypeStruct((owned, 2, rows, rows * feed_count), jnp.float32)
    own, near, mid, far, made = {}, {}, {}, {}, {}

    def launch(k):
        blocks = equalize(voltages, gain_cols, k, freq_count)
        arrived = lax.all_to_all(blocks, "freq", split_axis=0, concat_axis=0, tiled=True)
        own[k] = arrived.reshape(rows, 2 * samples)
        near[k] = lax.ppermute(own[k], "feed", INWARD + OUTWARD if k == 0 else INWARD)
        mid[k] = lax.ppermute(own[k], "feed", MIDDLE)
        far[k] = lax.ppermute(near[k], "feed", MIDDLE)

    def own_step(out, k):
        out = own_block(out, out_shape, k, place_own, own[k], own[k], "diag")
        return own_block(out, out_shape, k, place_near, own[k], near[k], "near") if k == 0 else out

    def near_step(out, k):
        out, rest = pair_block(out, k, place_near, own[k], near[k], near[k], own[k], "near")
        made[k, 1] = lax.ppermute(rest, "feed", OUTWARD)
        return out

    def mid_step(out, k):
        out, rest = pair_block(out, k, place_mid, own[k], near[k], mid[k], mid[k], "mid")
        made[k, 2] = lax.ppermute(rest, "feed", OUTWARD)
        return out

    def far_step(out, k):
        out, rest = pair_block(out, k, place_far, own[k], near[k], far[k], far[k], "far")
        made[k, 3] = lax.ppermute(rest, "feed", OUTWARD)
        return out

    def settle_step(out, *keys):
        columns = {1: near_mid, 2: far_mid, 3: far_end}
        return settle(out, is_mid, [(k, columns[b], made[k, b]) for k, b in keys])

    for k in range(owned):
        launch(k)
    out = own_step(None, 0)
    out = mid_step(out, 0)
    last = owned - 1
    for k in range(1, owned):
        out = own_step(out, k)
        out = near_step(out, k)
        out = mid_step(out, k)
        out = far_step(out, k - 1)
        if k >= 2:
            out = settle_step(out, *[(k - 2, b) for b in (1, 2, 3) if (k - 2, b) in made])
    out = far_step(out, last)
    if owned > 1:
        out = settle_step(out, *[(last - 1, b) for b in (1, 2, 3) if (last - 1, b) in made])
    out = settle_step(out, *[(last, b) for b in (1, 2) if (last, b) in made])
    return settle_step(out, (last, 3))


def stack_rows(own_rows, samples):
    real_part = own_rows[..., :samples]
    imag_part = own_rows[..., samples:]
    swapped = jnp.concatenate([imag_part, -real_part], axis=-1)
    return jnp.stack([own_rows, swapped], axis=1)


def per_device_gather(voltages, gains):
    channels, local_feeds, _, samples = voltages.shape
    freq_count = lax.axis_size("freq")
    owned = channels // freq_count
    gain_cols = jnp.transpose(gains, (1, 2, 0))
    results = []
    for k in range(owned):
        blocks = equalize(voltages, gain_cols, k, freq_count)
        arrived = lax.all_to_all(blocks, "freq", split_axis=0, concat_axis=0, tiled=True)
        own = arrived.reshape(freq_count * local_feeds, 2 * samples)
        columns = lax.all_gather(own, "feed", axis=0, tiled=True)
        product = jnp.einsum("qrk,fk->qrf", stack_rows(own[None], samples)[0], columns, preferred_element_type=jnp.float32)
        results.append(product * (1.0 / samples))
    return jnp.stack(results)


def solution(mesh):
    in_specs = (P(None, ("feed", "freq"), None, None), P(None, None, ("feed", "freq")))
    out_specs = P("freq", None, "feed", None)
    per_device = per_device_line if mesh.shape["feed"] == 4 else per_device_gather
    return jax.shard_map(
        per_device, mesh=mesh, in_specs=in_specs, out_specs=out_specs, check_vma=False
    )
```

time: 607 us -> 470 us (0.77)
  waiting for transfers between devices: 417 us -> 263 us
  Pallas kernels: 0 us -> 130 us
  blocking collectives: 76.7 us -> 0 us
  starting transfers between devices: 0.01 us -> 65.6 us
  other arithmetic: 44.7 us -> 4.81 us
  matrix products: 35.8 us -> 0 us
  local copies, waits for them, and re-layouts: 18.5 us -> 4.16 us
  between operations: 13.4 us -> 0.41 us
    all_gather x1 -> x0, waiting for transfers between devices: 417 us -> none  [per_device(): lax.all_gather(own_rows, 'feed', axis=1, tiled=True)]
    ppermute x0 -> x23, waiting for transfers between devices: none -> 228 us  [the longest x4 78.2 us: far_step(): made[k, 3] = lax.ppermute(rest, 'feed', OUTWARD)]
    pallas_call x0 -> x25, Pallas kernels: none -> 130 us  [the longest x11 54.9 us: pair_block(): pl.pallas_call(pair_kernel, grid_spec=pltpu.PrefetchScalarGridSpec(num_sc...]
    all_to_all x1 -> x0, blocking collectives: 76.7 us -> none  [per_device(): lax.all_to_all(blocks, 'freq', split_axis=0, concat_axis=2, tiled=True)]
    ppermute x0 -> x23, starting transfers between devices: none -> 48.9 us  [the longest x4 20.9 us: launch(): lax.ppermute(own[k], 'feed', INWARD + OUTWARD if k == 0 else INWARD)]
    another operation x3 -> x8, other arithmetic: 41.5 us -> 4.81 us  [the longest x4 2.45 us: settle(): jnp.stack([is_mid] + [column for _, column, _ in items]).astype(jnp.int32)]
    dot_general x1 -> x0, matrix products: 35.8 us -> none  [correlate(): jnp.einsum('cqrk,cfk->cqrf', stacked, columns, preferred_element_type=jnp...]
    all_to_all x0 -> x4, waiting for transfers between devices: none -> 35.5 us  [launch(): lax.all_to_all(blocks, 'freq', split_axis=0, concat_axis=0, tiled=True)]
  transfers between devices with their start and end apart: 1 -> 27, of which waited for: 1 -> 18; matrix products, arithmetic and copies ran while one was open for 1% -> 1% of each run, Pallas kernels for 0% -> 26%
where the time goes in v1:
time: 470 us; the launch traced here: 468 us
  waiting for transfers between devices  263 us (56%)
  Pallas kernels  130 us (28%)
  starting transfers between devices  65.6 us (14%)
  other arithmetic  4.81 us (1%)
    ppermute x4, waiting for transfers between devices, far_step(): made[k, 3] = lax.ppermute(rest, 'feed', OUTWARD)  78.2 us
    ppermute x3, waiting for transfers between devices, near_step(): made[k, 1] = lax.ppermute(rest, 'feed', OUTWARD)  63.7 us
    pallas_call x11, Pallas kernels, pair_block(): pl.pallas_call(pair_kernel, grid_spec=pltpu.PrefetchScalarGridSpec(num_sc...  54.9 us
    ppermute x4, waiting for transfers between devices, launch(): lax.ppermute(own[k], 'feed', INWARD + OUTWARD if k == 0 else INWARD)  47.4 us
    ppermute x4, waiting for transfers between devices, mid_step(): made[k, 2] = lax.ppermute(rest, 'feed', OUTWARD)  38.5 us
    all_to_all x4, waiting for transfers between devices, launch(): lax.all_to_all(blocks, 'freq', split_axis=0, concat_axis=0, tiled=True)  35.5 us
    pallas_call x5, Pallas kernels, own_block(): pl.pallas_call(own_kernel, grid_spec=pltpu.PrefetchScalarGridSpec(num_sca...  27.3 us
    pallas_call x4, Pallas kernels, equalize(): pl.pallas_call(equalize_kernel, grid=(freq_count,), in_specs=[pl.BlockSpe...  24.9 us
  transfers between devices with their start and end apart: 27, of which 18 were waited for; matrix products, arithmetic and copies ran while one was open for 1% of the time, Pallas kernels for 26%

profile of v1, /device:TPU:0, one launch (start us, length us, event | category | flops | bytes accessed | tf_op | source)
XLA Modules:
  0.0 468.0 jit_solution(345631957826925678)
XLA Ops:
  2.1 6.2 %equalize.6 = bf16[8,64,1536]{2,1,0:T(8,128)(2,1)} custom-call(s32[32,64,2,768]{3,2,1,0:T(2,128)} %volt_ref.7, f32[32,64,2]{2,1,0:T(8,128)} %bitcast.27), custom_call_target="tpu_custom_call" | custom-call | flops 4718592 | bytes 4718592 | tf_op jit(solution)/shard_map/equalize/pallas_call | solution.py:29
  8.4 5.2 %all-to-all-start.2 = ((bf16[8,64,1536]{2,1,0:T(8,128)(2,1)}), bf16[8,64,1536]{2,1,0:T(8,128)(2,1)}, u32[]{:S(2)}, u32[]{:S(2)}) async-start(bf16[8,64,1536]{2,1,0:T(8,128)(2,1)} %equalize.6), calls=%async_computation.2 | async-start | bytes 3145728 | tf_op jit(solution)/shard_map/all_to_all | solution.py:207
  13.6 6.2 %equalize.5 = bf16[8,64,1536]{2,1,0:T(8,128)(2,1)} custom-call(s32[32,64,2,768]{3,2,1,0:T(2,128)} %volt_ref.7, f32[32,64,2]{2,1,0:T(8,128)} %bitcast.28), custom_call_target="tpu_custom_call" | custom-call | flops 4718592 | bytes 4718592 | tf_op jit(solution)/shard_map/equalize/pallas_call | solution.py:29
  19.8 14.9 %all-to-all-done.2 = bf16[8,64,1536]{2,1,0:T(8,128)(2,1)} async-done(((bf16[8,64,1536]{2,1,0:T(8,128)(2,1)}), bf16[8,64,1536]{2,1,0:T(8,128)(2,1)}, u32[]{:S(2)}, u32[]{:S(2)}) %all-to-all-start.2) | async-done | bytes 1572896 | tf_op jit(solution)/shard_map/all_to_all | solution.py:207
  34.7 4.3 all-to-all-start.1
  39.0 6.2 %equalize.7 = bf16[8,64,1536]{2,1,0:T(8,128)(2,1)} custom-call(s32[32,64,2,768]{3,2,1,0:T(2,128)} %volt_ref.7, f32[32,64,2]{2,1,0:T(8,128)} %bitcast.29), custom_call_target="tpu_custom_call" | custom-call | flops 4718592 | bytes 4718592 | tf_op jit(solution)/shard_map/equalize/pallas_call | solution.py:29
  45.2 14.8 %all-to-all-done.1 = bf16[8,64,1536]{2,1,0:T(8,128)(2,1)} async-done(((bf16[8,64,1536]{2,1,0:T(8,128)(2,1)}), bf16[8,64,1536]{2,1,0:T(8,128)(2,1)}, u32[]{:S(2)}, u32[]{:S(2)}) %all-to-all-start.1) | async-done | bytes 1572896 | tf_op jit(solution)/shard_map/all_to_all | solution.py:207
  60.0 3.6 all-to-all-start.3
  67.5 6.4 %collective-permute-start.2 = (bf16[512,1536]{1,0:T(8,128)(2,1)}, bf16[512,1536]{1,0:T(8,128)(2,1)}, u32[]{:S(2)}, u32[]{:S(2)}) collective-permute-start(bf16[512,1536]{1,0:T(8,128)(2,1)} %bitcast.7.own_ref.other_ref.rest_other_ref), channel_id=1, source_target_pairs={{0,1},{3,2},{4,5},{7,6},{8,9},{11,10},{12,13},{15,14},{16,17},{19,... | collective-permute-start | bytes 4718600 | tf_op jit(solution)/shard_map/ppermute | solution.py:209
  73.9 6.2 %equalize.4 = bf16[8,64,1536]{2,1,0:T(8,128)(2,1)} custom-call(s32[32,64,2,768]{3,2,1,0:T(2,128)} %volt_ref.7, f32[32,64,2]{2,1,0:T(8,128)} %bitcast.30), custom_call_target="tpu_custom_call" | custom-call | flops 4718592 | bytes 4718592 | tf_op jit(solution)/shard_map/equalize/pallas_call | solution.py:29
  80.1 4.4 all-to-all-done.3
  84.5 3.6 all-to-all-start
  90.6 6.9 %collective-permute-start.9 = (bf16[512,1536]{1,0:T(8,128)(2,1)S(1)}, bf16[512,1536]{1,0:T(8,128)(2,1)}, u32[]{:S(2)}, u32[]{:S(2)}) collective-permute-start(bf16[512,1536]{1,0:T(8,128)(2,1)S(1)} %bitcast.19), channel_id=1, source_target_pairs={{0,1},{3,2},{4,5},{7,6},{8,9},{11,10},{12,13},{15,14},{16,17},{19,... | collective-permute-start | bytes 4718600 | tf_op jit(solution)/shard_map/ppermute | solution.py:209
  97.4 3.5 collective-permute-done.3.other_ref.end_ref
  109.0 25.5 %collective-permute-done.2.end_ref.other_ref = bf16[512,1536]{1,0:T(8,128)(2,1)} collective-permute-done((bf16[512,1536]{1,0:T(8,128)(2,1)}, bf16[512,1536]{1,0:T(8,128)(2,1)}, u32[]{:S(2)}, u32[]{:S(2)}) %collective-permute-start.2) | collective-permute-done | bytes 1572896 | tf_op jit(solution)/shard_map/ppermute | solution.py:209
  134.5 5.5 %collective-permute-start = (bf16[512,1536]{1,0:T(8,128)(2,1)S(1)}, bf16[512,1536]{1,0:T(8,128)(2,1)}, u32[]{:S(2)}, u32[]{:S(2)}) collective-permute-start(bf16[512,1536]{1,0:T(8,128)(2,1)S(1)} %bitcast.11), channel_id=1, source_target_pairs={{0,1},{3,2},{4,5},{7,6},{8,9},{11,10},{12,13},{15,14},{16,17},{19,... | collective-permute-start | bytes 4718600 | tf_op jit(solution)/shard_map/ppermute | solution.py:209
  140.1 5.4 %diag.4.refs_0_ = f32[4,2,512,2048]{3,2,1,0:T(8,128)} custom-call(s32[2]{0:T(128)} %pad_add_fusion.4.place_ref, bf16[512,1536]{1,0:T(8,128)(2,1)} %bitcast.9.own_ref.other_ref, bf16[512,1536]{1,0:T(8,128)(2,1)} %bitcast.9.own_ref.other_ref), custom_call_target="tpu_custom_call" | custom-call | flops 1610612736 | bytes 5242880 | tf_op jit(solution)/shard_map/diag/pallas_call | solution.py:75
  145.5 5.4 %near.4._ = f32[4,2,512,2048]{3,2,1,0:T(8,128)} custom-call(s32[2]{0:T(128)} %pad_add_fusion.3.place_ref, bf16[512,1536]{1,0:T(8,128)(2,1)} %bitcast.9.own_ref.other_ref, bf16[512,1536]{1,0:T(8,128)(2,1)} %collective-permute-done.3.other_ref.end_ref, f32[4,2,512,2048]{3,2,1,0:T(8,128)} %diag.4.refs_0_), custom_call_target="tpu_custom_call", output_to_operand_aliasing={{}: (3, {})} | custom-call | flops 1610612736 | bytes 5242880 | tf_op jit(solution)/shard_map/near/pallas_call | solution.py:75
  152.7 5.1 %mid.4 = (f32[4,2,512,2048]{3,2,1,0:T(8,128)}, bf16[2,512,512]{2,1,0:T(8,128)(2,1)}) custom-call(s32[2]{0:T(128)} %pad_add_fusion.5.place_ref, bf16[512,1536]{1,0:T(8,128)(2,1)} %bitcast.9.own_ref.other_ref, bf16[512,1536]{1,0:T(8,128)(2,1)} %collective-permute-done.3.other_ref.end_ref, ...), custom_call_target="tpu_custom_call", output_to_operand_aliasing={{0}: (5, {})} | custom-call | flops 3221225472 | bytes 9437184 | tf_op jit(solution)/shard_map/mid/pallas_call | solution.py:110
  157.8 5.5 %diag.5._ = f32[4,2,512,2048]{3,2,1,0:T(8,128)} custom-call(s32[2]{0:T(128)} %pad_add_fusion.4.place_ref, bf16[512,1536]{1,0:T(8,128)(2,1)} %bitcast.7.own_ref.other_ref.rest_other_ref, bf16[512,1536]{1,0:T(8,128)(2,1)} %bitcast.7.own_ref.other_ref.rest_other_ref, f32[4,2,512,2048]{3,2,1,0:T(8,128)} %get-tuple-element.27.refs_0_), custom_call_target="tpu_custom_call", output_to_operand_aliasing={{}: (3, {})} | custom-call | flops 1610612736 | bytes 5242880 | tf_op jit(solution)/shard_map/diag/pallas_call | solution.py:75
  163.3 5.1 %near.5 = (f32[4,2,512,2048]{3,2,1,0:T(8,128)}, bf16[2,512,512]{2,1,0:T(8,128)(2,1)}) custom-call(s32[2]{0:T(128)} %pad_add_fusion.3.place_ref, bf16[512,1536]{1,0:T(8,128)(2,1)} %bitcast.7.own_ref.other_ref.rest_other_ref, bf16[512,1536]{1,0:T(8,128)(2,1)} %collective-permute-done.2.end_ref.other_ref, ...), custom_call_target="tpu_custom_call", output_to_operand_aliasing={{0}: (5, {})} | custom-call | flops 3221225472 | bytes 9437184 | tf_op jit(solution)/shard_map/near/pallas_call | solution.py:110
  172.1 4.7 %mid.5 = (f32[4,2,512,2048]{3,2,1,0:T(8,128)}, bf16[2,512,512]{2,1,0:T(8,128)(2,1)}) custom-call(s32[2]{0:T(128)} %pad_add_fusion.5.place_ref, bf16[512,1536]{1,0:T(8,128)(2,1)} %bitcast.7.own_ref.other_ref.rest_other_ref, bf16[512,1536]{1,0:T(8,128)(2,1)} %collective-permute-done.2.end_ref.other_ref, ...), custom_call_target="tpu_custom_call", output_to_operand_aliasing={{0}: (5, {})} | custom-call | flops 3221225472 | bytes 9437184 | tf_op jit(solution)/shard_map/mid/pallas_call | solution.py:110
  176.8 4.7 %far.4 = (f32[4,2,512,2048]{3,2,1,0:T(8,128)}, bf16[2,512,512]{2,1,0:T(8,128)(2,1)}) custom-call(s32[2]{0:T(128)} %pad_add_fusion.1.place_ref, bf16[512,1536]{1,0:T(8,128)(2,1)} %bitcast.9.own_ref.other_ref, bf16[512,1536]{1,0:T(8,128)(2,1)} %collective-permute-done.3.other_ref.end_ref, ...), custom_call_target="tpu_custom_call", output_to_operand_aliasing={{0}: (5, {})} | custom-call | flops 3221225472 | bytes 9437184 | tf_op jit(solution)/shard_map/far/pallas_call | solution.py:110
  182.8 18.4 %collective-permute-done.end_ref.other_ref = bf16[512,1536]{1,0:T(8,128)(2,1)} collective-permute-done((bf16[512,1536]{1,0:T(8,128)(2,1)S(1)}, bf16[512,1536]{1,0:T(8,128)(2,1)}, u32[]{:S(2)}, u32[]{:S(2)}) %collective-permute-start) | collective-permute-done | bytes 1572896 | tf_op jit(solution)/shard_map/ppermute | solution.py:209
  202.7 5.5 %diag.6._ = f32[4,2,512,2048]{3,2,1,0:T(8,128)} custom-call(s32[2]{0:T(128)} %pad_add_fusion.4.place_ref, bf16[512,1536]{1,0:T(8,128)(2,1)} %bitcast.21, bf16[512,1536]{1,0:T(8,128)(2,1)} %bitcast.22, f32[4,2,512,2048]{3,2,1,0:T(8,128)} %get-tuple-element.32.refs_0_), custom_call_target="tpu_custom_call", output_to_operand_aliasing={{}: (3, {})} | custom-call | flops 1610612736 | bytes 5242880 | tf_op jit(solution)/shard_map/diag/pallas_call | solution.py:75
  208.2 5.1 %near.6 = (f32[4,2,512,2048]{3,2,1,0:T(8,128)}, bf16[2,512,512]{2,1,0:T(8,128)(2,1)}) custom-call(s32[2]{0:T(128)} %pad_add_fusion.3.place_ref, bf16[512,1536]{1,0:T(8,128)(2,1)} %bitcast.23, bf16[512,1536]{1,0:T(8,128)(2,1)} %collective-permute-done.9.end_ref.other_ref, ...), custom_call_target="tpu_custom_call", output_to_operand_aliasing={{0}: (5, {})} | custom-call | flops 3221225472 | bytes 9437184 | tf_op jit(solution)/shard_map/near/pallas_call | solution.py:110
  214.0 4.8 %mid.6 = (f32[4,2,512,2048]{3,2,1,0:T(8,128)}, bf16[2,512,512]{2,1,0:T(8,128)(2,1)}) custom-call(s32[2]{0:T(128)} %pad_add_fusion.5.place_ref, bf16[512,1536]{1,0:T(8,128)(2,1)} %bitcast.25, bf16[512,1536]{1,0:T(8,128)(2,1)} %collective-permute-done.9.end_ref.other_ref, ...), custom_call_target="tpu_custom_call", output_to_operand_aliasing={{0}: (5, {})} | custom-call | flops 3221225472 | bytes 9437184 | tf_op jit(solution)/shard_map/mid/pallas_call | solution.py:110
  218.8 5.2 %far.5 = (f32[4,2,512,2048]{3,2,1,0:T(8,128)}, bf16[2,512,512]{2,1,0:T(8,128)(2,1)}) custom-call(s32[2]{0:T(128)} %pad_add_fusion.1.place_ref, bf16[512,1536]{1,0:T(8,128)(2,1)} %bitcast.7.own_ref.other_ref.rest_other_ref, bf16[512,1536]{1,0:T(8,128)(2,1)} %collective-permute-done.2.end_ref.other_ref, ...), custom_call_target="tpu_custom_call", output_to_operand_aliasing={{0}: (5, {})} | custom-call | flops 3221225472 | bytes 9437184 | tf_op jit(solution)/shard_map/far/pallas_call | solution.py:110
  223.9 9.1 %collective-permute-done.15.refs_0_ = bf16[2,512,512]{2,1,0:T(8,128)(2,1)} collective-permute-done((bf16[2,512,512]{2,1,0:T(8,128)(2,1)}, bf16[2,512,512]{2,1,0:T(8,128)(2,1)}, u32[]{:S(2)}, u32[]{:S(2)}) %collective-permute-start.15) | collective-permute-done | bytes 1048608 | tf_op jit(solution)/shard_map/ppermute | solution.py:224
  234.3 19.3 %collective-permute-done.16.refs_1_ = bf16[2,512,512]{2,1,0:T(8,128)(2,1)} collective-permute-done((bf16[2,512,512]{2,1,0:T(8,128)(2,1)}, bf16[2,512,512]{2,1,0:T(8,128)(2,1)}, u32[]{:S(2)}, u32[]{:S(2)}) %collective-permute-start.16) | collective-permute-done | bytes 1048608 | tf_op jit(solution)/shard_map/ppermute | solution.py:229
  254.9 4.3 settle.5.refs_0_
  260.6 5.5 %diag.7._ = f32[4,2,512,2048]{3,2,1,0:T(8,128)} custom-call(s32[2]{0:T(128)} %pad_add_fusion.4.place_ref, bf16[512,1536]{1,0:T(8,128)(2,1)} %bitcast.13, bf16[512,1536]{1,0:T(8,128)(2,1)} %bitcast.14, f32[4,2,512,2048]{3,2,1,0:T(8,128)} %settle.5.refs_0_), custom_call_target="tpu_custom_call", output_to_operand_aliasing={{}: (3, {})} | custom-call | flops 1610612736 | bytes 5242880 | tf_op jit(solution)/shard_map/diag/pallas_call | solution.py:75
  267.3 5.1 %near.7 = (f32[4,2,512,2048]{3,2,1,0:T(8,128)}, bf16[2,512,512]{2,1,0:T(8,128)(2,1)}) custom-call(s32[2]{0:T(128)} %pad_add_fusion.3.place_ref, bf16[512,1536]{1,0:T(8,128)(2,1)} %bitcast.15, bf16[512,1536]{1,0:T(8,128)(2,1)} %collective-permute-done.end_ref.other_ref, ...), custom_call_target="tpu_custom_call", output_to_operand_aliasing={{0}: (5, {})} | custom-call | flops 3221225472 | bytes 9437184 | tf_op jit(solution)/shard_map/near/pallas_call | solution.py:110
  272.5 5.2 %mid.7 = (f32[4,2,512,2048]{3,2,1,0:T(8,128)}, bf16[2,512,512]{2,1,0:T(8,128)(2,1)}) custom-call(s32[2]{0:T(128)} %pad_add_fusion.5.place_ref, bf16[512,1536]{1,0:T(8,128)(2,1)} %bitcast.17, bf16[512,1536]{1,0:T(8,128)(2,1)} %collective-permute-done.end_ref.other_ref, ...), custom_call_target="tpu_custom_call", output_to_operand_aliasing={{0}: (5, {})} | custom-call | flops 3221225472 | bytes 9437184 | tf_op jit(solution)/shard_map/mid/pallas_call | solution.py:110
  277.7 5.2 %far.6 = (f32[4,2,512,2048]{3,2,1,0:T(8,128)}, bf16[2,512,512]{2,1,0:T(8,128)(2,1)}) custom-call(s32[2]{0:T(128)} %pad_add_fusion.1.place_ref, bf16[512,1536]{1,0:T(8,128)(2,1)} %bitcast.26, bf16[512,1536]{1,0:T(8,128)(2,1)} %collective-permute-done.9.end_ref.other_ref, ...), custom_call_target="tpu_custom_call", output_to_operand_aliasing={{0}: (5, {})} | custom-call | flops 3221225472 | bytes 9437184 | tf_op jit(solution)/shard_map/far/pallas_call | solution.py:110
  282.8 3.7 collective-permute-done.7.refs_1_
  287.9 21.2 %collective-permute-done.5.refs_0_ = bf16[2,512,512]{2,1,0:T(8,128)(2,1)} collective-permute-done((bf16[2,512,512]{2,1,0:T(8,128)(2,1)}, bf16[2,512,512]{2,1,0:T(8,128)(2,1)}, u32[]{:S(2)}, u32[]{:S(2)}) %collective-permute-start.5) | collective-permute-done | bytes 1048608 | tf_op jit(solution)/shard_map/ppermute | solution.py:219
  310.3 21.1 %collective-permute-done.12.refs_2_ = bf16[2,512,512]{2,1,0:T(8,128)(2,1)S(1)} collective-permute-done((bf16[2,512,512]{2,1,0:T(8,128)(2,1)}, bf16[2,512,512]{2,1,0:T(8,128)(2,1)S(1)}, u32[]{:S(2)}, u32[]{:S(2)}) %collective-permute-start.12) | collective-permute-done | bytes 1048608 | tf_op jit(solution)/shard_map/ppermute | solution.py:229
  333.7 5.3 %settle.6._ = f32[4,2,512,2048]{3,2,1,0:T(8,128)} custom-call(s32[4]{0:T(128)} %pad_add_fusion.2.place_ref, bf16[2,512,512]{2,1,0:T(8,128)(2,1)} %collective-permute-done.5.refs_0_, bf16[2,512,512]{2,1,0:T(8,128)(2,1)} %collective-permute-done.7.refs_1_, bf16[2,512,512]{2,1,0:T(8,128)(2,1)} %copy-done.5, ...), custom_call_target="tpu_custom_call", output_to_operand_aliasing={{}: (4, {})} | custom-call | flops 1572864 | bytes 9437184 | tf_op jit(solution)/shard_map/settle/pallas_call | solution.py:162
  340.6 4.8 %far.7 = (f32[4,2,512,2048]{3,2,1,0:T(8,128)}, bf16[2,512,512]{2,1,0:T(8,128)(2,1)}) custom-call(s32[2]{0:T(128)} %pad_add_fusion.1.place_ref, bf16[512,1536]{1,0:T(8,128)(2,1)} %bitcast.18, bf16[512,1536]{1,0:T(8,128)(2,1)} %collective-permute-done.end_ref.other_ref, bf16[512,1536]{1,0:T(8,128)(2,1)} %copy-done.2, ...), custom_call_target="tpu_custom_call", output_to_operand_aliasing={{0}: (5, {})} | custom-call | flops 3221225472 | bytes 9437184 | tf_op jit(solution)/shard_map/far/pallas_call | solution.py:110
  345.3 8.7 %collective-permute-done.21.refs_1_ = bf16[2,512,512]{2,1,0:T(8,128)(2,1)} collective-permute-done((bf16[2,512,512]{2,1,0:T(8,128)(2,1)}, bf16[2,512,512]{2,1,0:T(8,128)(2,1)}, u32[]{:S(2)}, u32[]{:S(2)}) %collective-permute-start.21) | collective-permute-done | bytes 1048608 | tf_op jit(solution)/shard_map/ppermute | solution.py:224
  356.5 20.0 %collective-permute-done.20.refs_0_ = bf16[2,512,512]{2,1,0:T(8,128)(2,1)} collective-permute-done((bf16[2,512,512]{2,1,0:T(8,128)(2,1)}, bf16[2,512,512]{2,1,0:T(8,128)(2,1)}, u32[]{:S(2)}, u32[]{:S(2)}) %collective-permute-start.20) | collective-permute-done | bytes 1048608 | tf_op jit(solution)/shard_map/ppermute | solution.py:219
  376.4 22.5 %collective-permute-done.22.refs_2_ = bf16[2,512,512]{2,1,0:T(8,128)(2,1)} collective-permute-done((bf16[2,512,512]{2,1,0:T(8,128)(2,1)}, bf16[2,512,512]{2,1,0:T(8,128)(2,1)}, u32[]{:S(2)}, u32[]{:S(2)}) %collective-permute-start.22) | collective-permute-done | bytes 1048608 | tf_op jit(solution)/shard_map/ppermute | solution.py:229
  398.9 5.3 %settle.7.refs_2_ = f32[4,2,512,2048]{3,2,1,0:T(8,128)} custom-call(s32[4]{0:T(128)} %pad_add_fusion.2.place_ref, bf16[2,512,512]{2,1,0:T(8,128)(2,1)} %collective-permute-done.20.refs_0_, bf16[2,512,512]{2,1,0:T(8,128)(2,1)} %collective-permute-done.21.refs_1_, ...), custom_call_target="tpu_custom_call", output_to_operand_aliasing={{}: (4, {})} | custom-call | flops 1572864 | bytes 9437184 | tf_op jit(solution)/shard_map/settle/pallas_call | solution.py:162
  404.2 17.1 %collective-permute-done.19.refs_1_ = bf16[2,512,512]{2,1,0:T(8,128)(2,1)S(1)} collective-permute-done((bf16[2,512,512]{2,1,0:T(8,128)(2,1)}, bf16[2,512,512]{2,1,0:T(8,128)(2,1)S(1)}, u32[]{:S(2)}, u32[]{:S(2)}) %collective-permute-start.19) | collective-permute-done | bytes 1048608 | tf_op jit(solution)/shard_map/ppermute | solution.py:224
  421.3 22.6 %collective-permute-done.18.refs_0_ = bf16[2,512,512]{2,1,0:T(8,128)(2,1)} collective-permute-done((bf16[2,512,512]{2,1,0:T(8,128)(2,1)}, bf16[2,512,512]{2,1,0:T(8,128)(2,1)}, u32[]{:S(2)}, u32[]{:S(2)}) %collective-permute-start.18) | collective-permute-done | bytes 1048608 | tf_op jit(solution)/shard_map/ppermute | solution.py:219
  443.9 4.3 settle.8.refs_1_
  448.2 15.4 %collective-permute-done.17.refs_0_ = bf16[2,512,512]{2,1,0:T(8,128)(2,1)S(1)} collective-permute-done((bf16[2,512,512]{2,1,0:T(8,128)(2,1)}, bf16[2,512,512]{2,1,0:T(8,128)(2,1)S(1)}, u32[]{:S(2)}, u32[]{:S(2)}) %collective-permute-start.17) | collective-permute-done | bytes 1048608 | tf_op jit(solution)/shard_map/ppermute | solution.py:229
  (52 shorter events, 43.9 us)
Async XLA Ops:
  8.4 26.3 %all-to-all-start.2 = ((bf16[8,64,1536]{2,1,0:T(8,128)(2,1)}), bf16[8,64,1536]{2,1,0:T(8,128)(2,1)}, u32[]{:S(2)}, u32[]{:S(2)}) async-start(bf16[8,64,1536]{2,1,0:T(8,128)(2,1)} %equalize.6), calls=%async_computation.2 | async-start | bytes 3145728 | tf_op jit(solution)/shard_map/all_to_all | solution.py:207
  34.7 25.3 %all-to-all-start.1 = ((bf16[8,64,1536]{2,1,0:T(8,128)(2,1)}), bf16[8,64,1536]{2,1,0:T(8,128)(2,1)}, u32[]{:S(2)}, u32[]{:S(2)}) async-start(bf16[8,64,1536]{2,1,0:T(8,128)(2,1)} %equalize.5), calls=%async_computation.1 | async-start | bytes 3145728 | tf_op jit(solution)/shard_map/all_to_all | solution.py:207
  60.0 24.5 %all-to-all-start.3 = ((bf16[8,64,1536]{2,1,0:T(8,128)(2,1)}), bf16[8,64,1536]{2,1,0:T(8,128)(2,1)S(1)}, u32[]{:S(2)}, u32[]{:S(2)}) async-start(bf16[8,64,1536]{2,1,0:T(8,128)(2,1)} %equalize.7), calls=%async_computation.3 | async-start | bytes 3145728 | tf_op jit(solution)/shard_map/all_to_all | solution.py:207
  63.6 37.4 %collective-permute-start.3 = (bf16[512,1536]{1,0:T(8,128)(2,1)}, bf16[512,1536]{1,0:T(8,128)(2,1)}, u32[]{:S(2)}, u32[]{:S(2)}) collective-permute-start(bf16[512,1536]{1,0:T(8,128)(2,1)} %bitcast.9.own_ref.other_ref), channel_id=1, source_target_pairs={{0,1},{3,2},{1,0},{2,3},{4,5},{7,6},{5,4},{6,7},{8,9},{11,10},{9,8... | collective-permute-start | bytes 4718600 | tf_op jit(solution)/shard_map/ppermute | solution.py:209
  65.7 40.0 %collective-permute-start.4 = (bf16[512,1536]{1,0:T(8,128)(2,1)}, bf16[512,1536]{1,0:T(8,128)(2,1)}, u32[]{:S(2)}, u32[]{:S(2)}) collective-permute-start(bf16[512,1536]{1,0:T(8,128)(2,1)} %bitcast.9.own_ref.other_ref), channel_id=1, source_target_pairs={{1,2},{2,1},{5,6},{6,5},{9,10},{10,9},{13,14},{14,13},{17,18},{18,... | collective-permute-start | bytes 4718600 | tf_op jit(solution)/shard_map/ppermute | solution.py:210
  67.5 67.0 %collective-permute-start.2 = (bf16[512,1536]{1,0:T(8,128)(2,1)}, bf16[512,1536]{1,0:T(8,128)(2,1)}, u32[]{:S(2)}, u32[]{:S(2)}) collective-permute-start(bf16[512,1536]{1,0:T(8,128)(2,1)} %bitcast.7.own_ref.other_ref.rest_other_ref), channel_id=1, source_target_pairs={{0,1},{3,2},{4,5},{7,6},{8,9},{11,10},{12,13},{15,14},{16,17},{19,... | collective-permute-start | bytes 4718600 | tf_op jit(solution)/shard_map/ppermute | solution.py:209
  84.5 66.4 %copy-start.1 = (bf16[8,64,1536]{2,1,0:T(8,128)(2,1)}, bf16[8,64,1536]{2,1,0:T(8,128)(2,1)S(1)}, u32[]{:S(2)}) copy-start(bf16[8,64,1536]{2,1,0:T(8,128)(2,1)S(1)} %all-to-all-done.3) | copy-start | bytes 4718596
  84.5 24.5 %all-to-all-start = ((bf16[8,64,1536]{2,1,0:T(8,128)(2,1)}), bf16[8,64,1536]{2,1,0:T(8,128)(2,1)S(1)}, u32[]{:S(2)}, u32[]{:S(2)}) async-start(bf16[8,64,1536]{2,1,0:T(8,128)(2,1)} %equalize.4), calls=%async_computation | async-start | bytes 3145728 | tf_op jit(solution)/shard_map/all_to_all | solution.py:207
  88.1 62.8 %collective-permute-start.6 = (bf16[512,1536]{1,0:T(8,128)(2,1)}, bf16[512,1536]{1,0:T(8,128)(2,1)}, u32[]{:S(2)}, u32[]{:S(2)}) collective-permute-start(bf16[512,1536]{1,0:T(8,128)(2,1)} %bitcast.7.own_ref.other_ref.rest_other_ref), channel_id=1, source_target_pairs={{1,2},{2,1},{5,6},{6,5},{9,10},{10,9},{13,14},{14,13},{17,18},{18,... | collective-permute-start | bytes 4718600 | tf_op jit(solution)/shard_map/ppermute | solution.py:210
  90.6 77.8 %collective-permute-start.9 = (bf16[512,1536]{1,0:T(8,128)(2,1)S(1)}, bf16[512,1536]{1,0:T(8,128)(2,1)}, u32[]{:S(2)}, u32[]{:S(2)}) collective-permute-start(bf16[512,1536]{1,0:T(8,128)(2,1)S(1)} %bitcast.19), channel_id=1, source_target_pairs={{0,1},{3,2},{4,5},{7,6},{8,9},{11,10},{12,13},{15,14},{16,17},{19,... | collective-permute-start | bytes 4718600 | tf_op jit(solution)/shard_map/ppermute | solution.py:209
  100.9 69.3 %collective-permute-start.11 = (bf16[512,1536]{1,0:T(8,128)(2,1)}, bf16[512,1536]{1,0:T(8,128)(2,1)}, u32[]{:S(2)}, u32[]{:S(2)}) collective-permute-start(bf16[512,1536]{1,0:T(8,128)(2,1)} %collective-permute-done.3.other_ref.end_ref), channel_id=1, source_target_pairs={{1,2},{2,1},{5,6},{6,5},{9,10},{10,9},{13,14},{14,13},{17,18},{18,... | collective-permute-start | bytes 4718600 | tf_op jit(solution)/shard_map/ppermute | solution.py:211
  105.7 75.8 %collective-permute-start.10 = (bf16[512,1536]{1,0:T(8,128)(2,1)S(1)}, bf16[512,1536]{1,0:T(8,128)(2,1)}, u32[]{:S(2)}, u32[]{:S(2)}) collective-permute-start(bf16[512,1536]{1,0:T(8,128)(2,1)S(1)} %bitcast.20), channel_id=1, source_target_pairs={{1,2},{2,1},{5,6},{6,5},{9,10},{10,9},{13,14},{14,13},{17,18},{18,... | collective-permute-start | bytes 4718600 | tf_op jit(solution)/shard_map/ppermute | solution.py:210
  109.0 59.4 %copy-start = (bf16[8,64,1536]{2,1,0:T(8,128)(2,1)}, bf16[8,64,1536]{2,1,0:T(8,128)(2,1)S(1)}, u32[]{:S(2)}) copy-start(bf16[8,64,1536]{2,1,0:T(8,128)(2,1)S(1)} %all-to-all-done) | copy-start | bytes 4718596
  134.5 66.7 %collective-permute-start = (bf16[512,1536]{1,0:T(8,128)(2,1)S(1)}, bf16[512,1536]{1,0:T(8,128)(2,1)}, u32[]{:S(2)}, u32[]{:S(2)}) collective-permute-start(bf16[512,1536]{1,0:T(8,128)(2,1)S(1)} %bitcast.11), channel_id=1, source_target_pairs={{0,1},{3,2},{4,5},{7,6},{8,9},{11,10},{12,13},{15,14},{16,17},{19,... | collective-permute-start | bytes 4718600 | tf_op jit(solution)/shard_map/ppermute | solution.py:209
  150.9 62.4 %collective-permute-start.8 = (bf16[512,1536]{1,0:T(8,128)(2,1)}, bf16[512,1536]{1,0:T(8,128)(2,1)}, u32[]{:S(2)}, u32[]{:S(2)}) collective-permute-start(bf16[512,1536]{1,0:T(8,128)(2,1)} %collective-permute-done.2.end_ref.other_ref), channel_id=1, source_target_pairs={{1,2},{2,1},{5,6},{6,5},{9,10},{10,9},{13,14},{14,13},{17,18},{18,... | collective-permute-start | bytes 4718600 | tf_op jit(solution)/shard_map/ppermute | solution.py:211
  168.4 90.9 %collective-permute-start.14 = (bf16[512,1536]{1,0:T(8,128)(2,1)S(1)}, bf16[512,1536]{1,0:T(8,128)(2,1)}, u32[]{:S(2)}, u32[]{:S(2)}) collective-permute-start(bf16[512,1536]{1,0:T(8,128)(2,1)S(1)} %bitcast.12), channel_id=1, source_target_pairs={{1,2},{2,1},{5,6},{6,5},{9,10},{10,9},{13,14},{14,13},{17,18},{18,... | collective-permute-start | bytes 4718600 | tf_op jit(solution)/shard_map/ppermute | solution.py:210
  170.2 95.8 %collective-permute-start.13 = (bf16[512,1536]{1,0:T(8,128)(2,1)}, bf16[512,1536]{1,0:T(8,128)(2,1)}, u32[]{:S(2)}, u32[]{:S(2)}) collective-permute-start(bf16[512,1536]{1,0:T(8,128)(2,1)} %collective-permute-done.9.end_ref.other_ref), channel_id=1, source_target_pairs={{1,2},{2,1},{5,6},{6,5},{9,10},{10,9},{13,14},{14,13},{17,18},{18,... | collective-permute-start | bytes 4718600 | tf_op jit(solution)/shard_map/ppermute | solution.py:211
  181.5 51.5 %collective-permute-start.15 = (bf16[2,512,512]{2,1,0:T(8,128)(2,1)}, bf16[2,512,512]{2,1,0:T(8,128)(2,1)}, u32[]{:S(2)}, u32[]{:S(2)}) collective-permute-start(bf16[2,512,512]{2,1,0:T(8,128)(2,1)} %get-tuple-element.36), channel_id=1, source_target_pairs={{1,0},{2,3},{5,4},{6,7},{9,8},{10,11},{13,12},{14,15},{17,16},{18,... | collective-permute-start | bytes 3145736 | tf_op jit(solution)/shard_map/ppermute | solution.py:224
  201.2 52.5 %collective-permute-start.16 = (bf16[2,512,512]{2,1,0:T(8,128)(2,1)}, bf16[2,512,512]{2,1,0:T(8,128)(2,1)}, u32[]{:S(2)}, u32[]{:S(2)}) collective-permute-start(bf16[2,512,512]{2,1,0:T(8,128)(2,1)} %get-tuple-element.37), channel_id=1, source_target_pairs={{1,0},{2,3},{5,4},{6,7},{9,8},{10,11},{13,12},{14,15},{17,16},{18,... | collective-permute-start | bytes 3145736 | tf_op jit(solution)/shard_map/ppermute | solution.py:229
  213.3 125.8 %collective-permute-start.1 = (bf16[512,1536]{1,0:T(8,128)(2,1)}, bf16[512,1536]{1,0:T(8,128)(2,1)S(1)}, u32[]{:S(2)}, u32[]{:S(2)}) collective-permute-start(bf16[512,1536]{1,0:T(8,128)(2,1)} %collective-permute-done.end_ref.other_ref), channel_id=1, source_target_pairs={{1,2},{2,1},{5,6},{6,5},{9,10},{10,9},{13,14},{14,13},{17,18},{18,... | collective-permute-start | bytes 4718600 | tf_op jit(solution)/shard_map/ppermute | solution.py:211
  233.0 53.5 %collective-permute-start.7 = (bf16[2,512,512]{2,1,0:T(8,128)(2,1)}, bf16[2,512,512]{2,1,0:T(8,128)(2,1)}, u32[]{:S(2)}, u32[]{:S(2)}) collective-permute-start(bf16[2,512,512]{2,1,0:T(8,128)(2,1)} %get-tuple-element.30), channel_id=1, source_target_pairs={{1,0},{2,3},{5,4},{6,7},{9,8},{10,11},{13,12},{14,15},{17,16},{18,... | collective-permute-start | bytes 3145736 | tf_op jit(solution)/shard_map/ppermute | solution.py:224
  253.7 55.4 %collective-permute-start.5 = (bf16[2,512,512]{2,1,0:T(8,128)(2,1)}, bf16[2,512,512]{2,1,0:T(8,128)(2,1)}, u32[]{:S(2)}, u32[]{:S(2)}) collective-permute-start(bf16[2,512,512]{2,1,0:T(8,128)(2,1)} %get-tuple-element.28), channel_id=1, source_target_pairs={{1,0},{2,3},{5,4},{6,7},{9,8},{10,11},{13,12},{14,15},{17,16},{18,... | collective-permute-start | bytes 3145736 | tf_op jit(solution)/shard_map/ppermute | solution.py:219
  259.3 72.1 %collective-permute-start.12 = (bf16[2,512,512]{2,1,0:T(8,128)(2,1)}, bf16[2,512,512]{2,1,0:T(8,128)(2,1)S(1)}, u32[]{:S(2)}, u32[]{:S(2)}) collective-permute-start(bf16[2,512,512]{2,1,0:T(8,128)(2,1)} %get-tuple-element.35), channel_id=1, source_target_pairs={{1,0},{2,3},{5,4},{6,7},{9,8},{10,11},{13,12},{14,15},{17,16},{18,... | collective-permute-start | bytes 3145736 | tf_op jit(solution)/shard_map/ppermute | solution.py:229
  266.1 87.9 %collective-permute-start.21 = (bf16[2,512,512]{2,1,0:T(8,128)(2,1)}, bf16[2,512,512]{2,1,0:T(8,128)(2,1)}, u32[]{:S(2)}, u32[]{:S(2)}) collective-permute-start(bf16[2,512,512]{2,1,0:T(8,128)(2,1)} %get-tuple-element.46), channel_id=1, source_target_pairs={{1,0},{2,3},{5,4},{6,7},{9,8},{10,11},{13,12},{14,15},{17,16},{18,... | collective-permute-start | bytes 3145736 | tf_op jit(solution)/shard_map/ppermute | solution.py:224
  286.6 89.9 %collective-permute-start.20 = (bf16[2,512,512]{2,1,0:T(8,128)(2,1)}, bf16[2,512,512]{2,1,0:T(8,128)(2,1)}, u32[]{:S(2)}, u32[]{:S(2)}) collective-permute-start(bf16[2,512,512]{2,1,0:T(8,128)(2,1)} %get-tuple-element.45), channel_id=1, source_target_pairs={{1,0},{2,3},{5,4},{6,7},{9,8},{10,11},{13,12},{14,15},{17,16},{18,... | collective-permute-start | bytes 3145736 | tf_op jit(solution)/shard_map/ppermute | solution.py:219
  309.0 89.9 %collective-permute-start.22 = (bf16[2,512,512]{2,1,0:T(8,128)(2,1)}, bf16[2,512,512]{2,1,0:T(8,128)(2,1)}, u32[]{:S(2)}, u32[]{:S(2)}) collective-permute-start(bf16[2,512,512]{2,1,0:T(8,128)(2,1)} %get-tuple-element.47), channel_id=1, source_target_pairs={{1,0},{2,3},{5,4},{6,7},{9,8},{10,11},{13,12},{14,15},{17,16},{18,... | collective-permute-start | bytes 3145736 | tf_op jit(solution)/shard_map/ppermute | solution.py:229
  331.4 1.0 copy-start.5
  332.4 88.9 %collective-permute-start.19 = (bf16[2,512,512]{2,1,0:T(8,128)(2,1)}, bf16[2,512,512]{2,1,0:T(8,128)(2,1)S(1)}, u32[]{:S(2)}, u32[]{:S(2)}) collective-permute-start(bf16[2,512,512]{2,1,0:T(8,128)(2,1)} %get-tuple-element.44), channel_id=1, source_target_pairs={{1,0},{2,3},{5,4},{6,7},{9,8},{10,11},{13,12},{14,15},{17,16},{18,... | collective-permute-start | bytes 3145736 | tf_op jit(solution)/shard_map/ppermute | solution.py:224
  339.0 1.5 copy-start.2
  339.0 104.8 %collective-permute-start.18 = (bf16[2,512,512]{2,1,0:T(8,128)(2,1)}, bf16[2,512,512]{2,1,0:T(8,128)(2,1)}, u32[]{:S(2)}, u32[]{:S(2)}) collective-permute-start(bf16[2,512,512]{2,1,0:T(8,128)(2,1)} %get-tuple-element.43), channel_id=1, source_target_pairs={{1,0},{2,3},{5,4},{6,7},{9,8},{10,11},{13,12},{14,15},{17,16},{18,... | collective-permute-start | bytes 3145736 | tf_op jit(solution)/shard_map/ppermute | solution.py:219
  354.0 109.6 %collective-permute-start.17 = (bf16[2,512,512]{2,1,0:T(8,128)(2,1)}, bf16[2,512,512]{2,1,0:T(8,128)(2,1)S(1)}, u32[]{:S(2)}, u32[]{:S(2)}) collective-permute-start(bf16[2,512,512]{2,1,0:T(8,128)(2,1)} %get-tuple-element.42), channel_id=1, source_target_pairs={{1,0},{2,3},{5,4},{6,7},{9,8},{10,11},{13,12},{14,15},{17,16},{18,... | collective-permute-start | bytes 3145736 | tf_op jit(solution)/shard_map/ppermute | solution.py:229
  421.3 22.6 %copy-start.3 = (bf16[2,512,512]{2,1,0:T(8,128)(2,1)}, bf16[2,512,512]{2,1,0:T(8,128)(2,1)S(1)}, u32[]{:S(2)}) copy-start(bf16[2,512,512]{2,1,0:T(8,128)(2,1)S(1)} %collective-permute-done.19.refs_1_) | copy-start | bytes 3145732
  463.5 1.0 copy-start.4

commit v2 on v1

--- a/solution.py
+++ b/solution.py
@@ -7,34 +7,54 @@
 from jax.experimental.pallas import tpu as pltpu
 from jax.sharding import PartitionSpec as P
 
+
 CONTRACT_LAST = (((1,), (1,)), ((), ()))
 INWARD = ((0, 1), (3, 2))
 MIDDLE = ((1, 2), (2, 1))
 OUTWARD = ((1, 0), (2, 3))
-
-
-def equalize_kernel(volt_ref, gain_ref, out_ref):
-    samples = volt_ref.shape[-1]
-    gain_real = gain_ref[0, :, 0:1]
-    gain_imag = gain_ref[0, :, 1:2]
-    volt_real = volt_ref[0, :, 0, :].astype(jnp.float32)
-    volt_imag = volt_ref[0, :, 1, :].astype(jnp.float32)
-    out_ref[0, :, :samples] = (gain_real * volt_real - gain_imag * volt_imag).astype(jnp.bfloat16)
-    out_ref[0, :, samples:] = (gain_real * volt_imag + gain_imag * volt_real).astype(jnp.bfloat16)
+SWAPPED_CHUNKS = 2
+
+
+def equalize_kernel(chunk, owned, volt_ref, gain_ref, out_ref, volt_buf, out_buf, in_sems, out_sems):
+    parts, _, _, samples = volt_buf.shape
+    loads = []
+    for f in range(parts):
+        load = pltpu.make_async_copy(volt_ref.at[f * owned + chunk], volt_buf.at[f], in_sems.at[f])
+        load.start()
+        loads.append(load)
+    gain_real = jnp.transpose(gain_ref[0])
+    gain_imag = jnp.transpose(gain_ref[1])
+    stores = []
+    for f in range(parts):
+        c = f * owned + chunk
+        real_col = gain_real[:, c:c + 1]
+        imag_col = gain_imag[:, c:c + 1]
+        loads[f].wait()
+        volt_real = volt_buf[f, :, 0, :].astype(jnp.float32)
+        volt_imag = volt_buf[f, :, 1, :].astype(jnp.float32)
+        out_buf[f, :, :samples] = (real_col * volt_real - imag_col * volt_imag).astype(jnp.bfloat16)
+        out_buf[f, :, samples:] = (real_col * volt_imag + imag_col * volt_real).astype(jnp.bfloat16)
+        store = pltpu.make_async_copy(out_buf.at[f], out_ref.at[f], out_sems.at[f])
+        store.start()
+        stores.append(store)
+    for store in stores:
+        store.wait()
 
 
 def equalize(voltages, gains, chunk, freq_count):
     channels, feeds, _, samples = voltages.shape
-    owned = channels // freq_count
+    shape = (freq_count, feeds, 2 * samples)
     return pl.pallas_call(
-        equalize_kernel,
-        grid=(freq_count,),
-        in_specs=[
-            pl.BlockSpec((1, feeds, 2, samples), lambda f: (f * owned + chunk, 0, 0, 0)),
-            pl.BlockSpec((1, feeds, 2), lambda f: (f * owned + chunk, 0, 0)),
+        functools.partial(equalize_kernel, chunk, channels // freq_count),
+        in_specs=[pl.BlockSpec(memory_space=pl.ANY), pl.BlockSpec(memory_space=pltpu.VMEM)],
+        out_specs=pl.BlockSpec(memory_space=pl.ANY),
+        out_shape=jax.ShapeDtypeStruct(shape, jnp.bfloat16),
+        scratch_shapes=[
+            pltpu.VMEM((freq_count, feeds, 2, samples), jnp.int32),
+            pltpu.VMEM(shape, jnp.bfloat16),
+            pltpu.SemaphoreType.DMA((freq_count,)),
+            pltpu.SemaphoreType.DMA((freq_count,)),
         ],
-        out_specs=pl.BlockSpec((1, feeds, 2 * samples), lambda f: (f, 0, 0)),
-        out_shape=jax.ShapeDtypeStruct((freq_count, feeds, 2 * samples), jnp.bfloat16),
         cost_estimate=pl.CostEstimate(
             flops=6 * freq_count * feeds * samples * 2,
             bytes_accessed=freq_count * feeds * samples * 12,
@@ -59,7 +79,7 @@
     out_ref[0, 1] = imag_part
 
 
-def own_block(out, out_shape, chunk, place, own, other, name):
+def own_block(out, out_shape, chunk, place, own, other):
     rows, depth = own.shape
     half = rows // 2
     in_specs = [
@@ -85,7 +105,6 @@
         cost_estimate=pl.CostEstimate(
             flops=4 * rows * rows * depth, bytes_accessed=4 * rows * depth + 8 * rows * rows, transcendentals=0
         ),
-        name=name,
     )(place, *operands)
 
 
@@ -102,7 +121,7 @@
         rest_ref[1] = imag_part.astype(jnp.bfloat16)
 
 
-def pair_block(out, chunk, place, own, end, other, rest_other, name):
+def pair_block(out, chunk, place, own, end, other, rest_other):
     rows, depth = own.shape
     half = rows // 2
     whole = pl.BlockSpec((rows, depth), lambda j, p: (0, 0))
@@ -126,7 +145,6 @@
         cost_estimate=pl.CostEstimate(
             flops=8 * rows * rows * depth, bytes_accessed=8 * rows * depth + 12 * rows * rows, transcendentals=0
         ),
-        name=name,
     )(place, own, end, other, rest_other, out)
 
 
@@ -198,58 +216,57 @@
     place_near = jnp.stack([jnp.where(is_mid == 1, near_end, near_mid), is_mid]).astype(jnp.int32)
     place_mid = jnp.stack([far_mid, is_mid]).astype(jnp.int32)
     place_far = jnp.stack([far_end, is_mid]).astype(jnp.int32)
-    gain_cols = jnp.transpose(gains, (1, 2, 0))
     out_shape = jax.ShapeDtypeStruct((owned, 2, rows, rows * feed_count), jnp.float32)
     own, near, mid, far, made = {}, {}, {}, {}, {}
 
-    def launch(k):
-        blocks = equalize(voltages, gain_cols, k, freq_count)
+    def permute(value, pairs):
+        return lax.ppermute(value, "feed", pairs)
+
+    for k in range(owned):
+        blocks = equalize(voltages, gains, k, freq_count)
         arrived = lax.all_to_all(blocks, "freq", split_axis=0, concat_axis=0, tiled=True)
         own[k] = arrived.reshape(rows, 2 * samples)
-        near[k] = lax.ppermute(own[k], "feed", INWARD + OUTWARD if k == 0 else INWARD)
-        mid[k] = lax.ppermute(own[k], "feed", MIDDLE)
-        far[k] = lax.ppermute(near[k], "feed", MIDDLE)
-
-    def own_step(out, k):
-        out = own_block(out, out_shape, k, place_own, own[k], own[k], "diag")
-        return own_block(out, out_shape, k, place_near, own[k], near[k], "near") if k == 0 else out
-
-    def near_step(out, k):
-        out, rest = pair_block(out, k, place_near, own[k], near[k], near[k], own[k], "near")
-        made[k, 1] = lax.ppermute(rest, "feed", OUTWARD)
-        return out
-
-    def mid_step(out, k):
-        out, rest = pair_block(out, k, place_mid, own[k], near[k], mid[k], mid[k], "mid")
-        made[k, 2] = lax.ppermute(rest, "feed", OUTWARD)
-        return out
-
-    def far_step(out, k):
-        out, rest = pair_block(out, k, place_far, own[k], near[k], far[k], far[k], "far")
-        made[k, 3] = lax.ppermute(rest, "feed", OUTWARD)
-        return out
-
-    def settle_step(out, *keys):
-        columns = {1: near_mid, 2: far_mid, 3: far_end}
-        return settle(out, is_mid, [(k, columns[b], made[k, b]) for k, b in keys])
-
-    for k in range(owned):
-        launch(k)
-    out = own_step(None, 0)
-    out = mid_step(out, 0)
+        near[k] = permute(own[k], INWARD + OUTWARD if k < SWAPPED_CHUNKS else INWARD)
+        mid[k] = permute(own[k], MIDDLE)
+        far[k] = permute(near[k], MIDDLE)
+
+    columns = {1: near_mid, 2: far_mid, 3: far_end}
+    out = None
+    for step in steps(owned):
+        kind, k = step[0], step[1]
+        if kind == "diag":
+            out = own_block(out, out_shape, k, place_own, own[k], own[k])
+        elif kind == "near" and k < SWAPPED_CHUNKS:
+            out = own_block(out, out_shape, k, place_near, own[k], near[k])
+        elif kind == "near":
+            out, rest = pair_block(out, k, place_near, own[k], near[k], near[k], own[k])
+            made[k, 1] = permute(rest, OUTWARD)
+        elif kind == "mid":
+            out, rest = pair_block(out, k, place_mid, own[k], near[k], mid[k], mid[k])
+            made[k, 2] = permute(rest, OUTWARD)
+        elif kind == "end":
+            out, rest = pair_block(out, k, place_far, own[k], near[k], far[k], far[k])
+            made[k, 3] = permute(rest, OUTWARD)
+        elif kind == "settle":
+            items = [(c, columns[b], made[c, b]) for c, b in step[2] if (c, b) in made]
+            out = settle(out, is_mid, items)
+    return out
+
+
+def steps(owned):
+    order = []
+    for k in range(owned + 1):
+        if k < owned:
+            order += [("diag", k), ("near", k), ("mid", k)]
+        if k >= 1:
+            if k == owned:
+                order += [("settle", j, [(j, 1), (j, 2), (j, 3)]) for j in range(owned - 2)]
+            order += [("end", k - 1)]
     last = owned - 1
-    for k in range(1, owned):
-        out = own_step(out, k)
-        out = near_step(out, k)
-        out = mid_step(out, k)
-        out = far_step(out, k - 1)
-        if k >= 2:
-            out = settle_step(out, *[(k - 2, b) for b in (1, 2, 3) if (k - 2, b) in made])
-    out = far_step(out, last)
-    if owned > 1:
-        out = settle_step(out, *[(last - 1, b) for b in (1, 2, 3) if (last - 1, b) in made])
-    out = settle_step(out, *[(last, b) for b in (1, 2) if (last, b) in made])
-    return settle_step(out, (last, 3))
+    order += [("settle", last - 1, [(last - 1, b) for b in (1, 2, 3)])]
+    order += [("settle", last, [(last, 1), (last, 2)])]
+    order += [("settle", owned, [(last, 3)])]
+    return order
 
 
 def stack_rows(own_rows, samples):
@@ -263,10 +280,9 @@
     channels, local_feeds, _, samples = voltages.shape
     freq_count = lax.axis_size("freq")
     owned = channels // freq_count
-    gain_cols = jnp.transpose(gains, (1, 2, 0))
     results = []
     for k in range(owned):
-        blocks = equalize(voltages, gain_cols, k, freq_count)
+        blocks = equalize(voltages, gains, k, freq_count)
         arrived = lax.all_to_all(blocks, "freq", split_axis=0, concat_axis=0, tiled=True)
         own = arrived.reshape(freq_count * local_feeds, 2 * samples)
         columns = lax.all_gather(own, "feed", axis=0, tiled=True)
@@ -278,7 +294,7 @@
 def solution(mesh):
     in_specs = (P(None, ("feed", "freq"), None, None), P(None, None, ("feed", "freq")))
     out_specs = P("freq", None, "feed", None)
-    per_device = per_device_line if mesh.shape["feed"] == 4 else per_device_gather
-    return jax.shard_map(
-        per_device, mesh=mesh, in_specs=in_specs, out_specs=out_specs, check_vma=False
-    )
+    on_line = mesh.shape["feed"] == 4
+    per_device = per_device_line if on_line else per_device_gather
+
+    return jax.shard_map(per_device, mesh=mesh, in_specs=in_specs, out_specs=out_specs, check_vma=False)

time: 470 us -> 468 us (level)
  waiting for transfers between devices: 263 us -> 280 us
  Pallas kernels: 130 us -> 120 us
  starting transfers between devices: 65.6 us -> 59.3 us
    ppermute x23 -> x22, waiting for transfers between devices: 228 us -> 238 us  [permute(): return lax.ppermute(value, 'feed', pairs)]
    pallas_call x4, Pallas kernels: 24.9 us -> 15.3 us  [equalize(): pl.pallas_call(functools.partial(equalize_kernel, chunk, channels // freq...]
    all_to_all x4, waiting for transfers between devices: 35.5 us -> 42.5 us  [per_device_line(): lax.all_to_all(blocks, 'freq', split_axis=0, concat_axis=0, tiled=True)]
    ppermute x23 -> x22, starting transfers between devices: 48.9 us -> 42.6 us  [permute(): return lax.ppermute(value, 'feed', pairs)]
    pallas_call x5 -> x6, Pallas kernels: 27.3 us -> 32.8 us  [own_block(): pl.pallas_call(own_kernel, grid_spec=pltpu.PrefetchScalarGridSpec(num_sca...]
    pallas_call x11 -> x10, Pallas kernels: 54.9 us -> 50.2 us  [pair_block(): pl.pallas_call(pair_kernel, grid_spec=pltpu.PrefetchScalarGridSpec(num_sc...]
  transfers between devices with their start and end apart: 27 -> 26, of which waited for: 18 -> 16; matrix products, arithmetic and copies ran while one was open for 1% -> 1% of each run, Pallas kernels for 26% -> 24%
where the time goes in v2:
time: 468 us; the launch traced here: 467 us
  waiting for transfers between devices  280 us (60%)
  Pallas kernels  120 us (26%)
  starting transfers between devices  59.3 us (13%)
  other arithmetic  4.94 us (1%)
    ppermute x22, waiting for transfers between devices, permute(): return lax.ppermute(value, 'feed', pairs)  238 us
    pallas_call x10, Pallas kernels, pair_block(): pl.pallas_call(pair_kernel, grid_spec=pltpu.PrefetchScalarGridSpec(num_sc...  50.2 us
    ppermute x22, starting transfers between devices, permute(): return lax.ppermute(value, 'feed', pairs)  42.6 us
    all_to_all x4, waiting for transfers between devices, per_device_line(): lax.all_to_all(blocks, 'freq', split_axis=0, concat_axis=0, tiled=True)  42.5 us
    pallas_call x6, Pallas kernels, own_block(): pl.pallas_call(own_kernel, grid_spec=pltpu.PrefetchScalarGridSpec(num_sca...  32.8 us
    pallas_call x5, Pallas kernels, settle(): pl.pallas_call(functools.partial(settle_kernel, chunks, rows), grid_spec=...  21.5 us
    all_to_all x4, starting transfers between devices, per_device_line(): lax.all_to_all(blocks, 'freq', split_axis=0, concat_axis=0, tiled=True)  16.7 us
    pallas_call x4, Pallas kernels, equalize(): pl.pallas_call(functools.partial(equalize_kernel, chunk, channels // freq...  15.3 us
  transfers between devices with their start and end apart: 26, of which 16 were waited for; matrix products, arithmetic and copies ran while one was open for 1% of the time, Pallas kernels for 24%

profile of v2, /device:TPU:0, one launch (start us, length us, event | category | flops | bytes accessed | tf_op | source)
XLA Modules:
  0.0 467.0 jit_solution(9066843491534160457)
XLA Ops:
  0.0 3.8 equalize.6
  3.8 5.2 %all-to-all-start.2 = ((bf16[8,64,1536]{2,1,0:T(8,128)(2,1)}), bf16[8,64,1536]{2,1,0:T(8,128)(2,1)}, u32[]{:S(2)}, u32[]{:S(2)}) async-start(bf16[8,64,1536]{2,1,0:T(8,128)(2,1)} %equalize.6), calls=%async_computation.2 | async-start | bytes 3145728 | tf_op jit(solution)/shard_map/all_to_all | solution.py:227
  9.1 3.8 equalize.5
  12.9 17.3 %all-to-all-done.2 = bf16[8,64,1536]{2,1,0:T(8,128)(2,1)} async-done(((bf16[8,64,1536]{2,1,0:T(8,128)(2,1)}), bf16[8,64,1536]{2,1,0:T(8,128)(2,1)}, u32[]{:S(2)}, u32[]{:S(2)}) %all-to-all-start.2) | async-done | bytes 1572896 | tf_op jit(solution)/shard_map/all_to_all | solution.py:227
  30.2 4.3 all-to-all-start.1
  34.5 3.8 equalize.7
  38.3 17.2 %all-to-all-done.1 = bf16[8,64,1536]{2,1,0:T(8,128)(2,1)} async-done(((bf16[8,64,1536]{2,1,0:T(8,128)(2,1)}), bf16[8,64,1536]{2,1,0:T(8,128)(2,1)}, u32[]{:S(2)}, u32[]{:S(2)}) %all-to-all-start.1) | async-done | bytes 1572896 | tf_op jit(solution)/shard_map/all_to_all | solution.py:227
  55.5 3.6 all-to-all-start.3
  59.1 2.1 collective-permute-start.4
  63.0 3.3 collective-permute-start.2
  68.2 3.8 equalize.4
  72.0 8.0 %all-to-all-done.3 = bf16[8,64,1536]{2,1,0:T(8,128)(2,1)S(1)} async-done(((bf16[8,64,1536]{2,1,0:T(8,128)(2,1)}), bf16[8,64,1536]{2,1,0:T(8,128)(2,1)S(1)}, u32[]{:S(2)}, u32[]{:S(2)}) %all-to-all-start.3) | async-done | bytes 1572896 | tf_op jit(solution)/shard_map/all_to_all | solution.py:227
  80.0 3.6 all-to-all-start
  83.6 5.2 %collective-permute-start.8 = (bf16[512,1536]{1,0:T(8,128)(2,1)S(1)}, bf16[512,1536]{1,0:T(8,128)(2,1)}, u32[]{:S(2)}, u32[]{:S(2)}) collective-permute-start(bf16[512,1536]{1,0:T(8,128)(2,1)S(1)} %bitcast.18), channel_id=1, source_target_pairs={{0,1},{3,2},{4,5},{7,6},{8,9},{11,10},{12,13},{15,14},{16,17},{19,... | collective-permute-start | bytes 4718600 | tf_op jit(solution)/shard_map/ppermute | solution.py:223
  88.8 8.0 %collective-permute-done.4.other_ref.end_ref = bf16[512,1536]{1,0:T(8,128)(2,1)} collective-permute-done((bf16[512,1536]{1,0:T(8,128)(2,1)}, bf16[512,1536]{1,0:T(8,128)(2,1)}, u32[]{:S(2)}, u32[]{:S(2)}) %collective-permute-start.4) | collective-permute-done | bytes 1572896 | tf_op jit(solution)/shard_map/ppermute | solution.py:223
  101.0 5.5 %shard_map.28.refs_0_ = f32[4,2,512,2048]{3,2,1,0:T(8,128)} custom-call(s32[2]{0:T(128)} %pad_add_fusion.5.place_ref, bf16[512,1536]{1,0:T(8,128)(2,1)} %bitcast.7.own_ref.other_ref, bf16[512,1536]{1,0:T(8,128)(2,1)} %bitcast.7.own_ref.other_ref), custom_call_target="tpu_custom_call" | custom-call | flops 1610612736 | bytes 5242880 | tf_op jit(solution)/shard_map/pallas_call | solution.py:95
  106.5 5.4 %shard_map.29._ = f32[4,2,512,2048]{3,2,1,0:T(8,128)} custom-call(s32[2]{0:T(128)} %pad_add_fusion.4.place_ref, bf16[512,1536]{1,0:T(8,128)(2,1)} %bitcast.7.own_ref.other_ref, bf16[512,1536]{1,0:T(8,128)(2,1)} %collective-permute-done.4.other_ref.end_ref, f32[4,2,512,2048]{3,2,1,0:T(8,128)} %shard_map.28.refs_0_), custom_call_target="tpu_custom_call", output_to_operand_aliasing={{}: (3, {})} | custom-call | flops 1610612736 | bytes 5242880 | tf_op jit(solution)/shard_map/pallas_call | solution.py:95
  113.7 5.2 %shard_map.30 = (f32[4,2,512,2048]{3,2,1,0:T(8,128)}, bf16[2,512,512]{2,1,0:T(8,128)(2,1)}) custom-call(s32[2]{0:T(128)} %pad_add_fusion.3.place_ref, bf16[512,1536]{1,0:T(8,128)(2,1)} %bitcast.7.own_ref.other_ref, bf16[512,1536]{1,0:T(8,128)(2,1)} %collective-permute-done.4.other_ref.end_ref, ...), custom_call_target="tpu_custom_call", output_to_operand_aliasing={{0}: (5, {})} | custom-call | flops 3221225472 | bytes 9437184 | tf_op jit(solution)/shard_map/pallas_call | solution.py:129
  118.9 11.3 %collective-permute-done.2.other_ref.end_ref = bf16[512,1536]{1,0:T(8,128)(2,1)} collective-permute-done((bf16[512,1536]{1,0:T(8,128)(2,1)}, bf16[512,1536]{1,0:T(8,128)(2,1)}, u32[]{:S(2)}, u32[]{:S(2)}) %collective-permute-start.2) | collective-permute-done | bytes 1572896 | tf_op jit(solution)/shard_map/ppermute | solution.py:223
  130.1 5.4 %collective-permute-start = (bf16[512,1536]{1,0:T(8,128)(2,1)S(1)}, bf16[512,1536]{1,0:T(8,128)(2,1)}, u32[]{:S(2)}, u32[]{:S(2)}) collective-permute-start(bf16[512,1536]{1,0:T(8,128)(2,1)S(1)} %bitcast.10), channel_id=1, source_target_pairs={{0,1},{3,2},{4,5},{7,6},{8,9},{11,10},{12,13},{15,14},{16,17},{19,... | collective-permute-start | bytes 4718600 | tf_op jit(solution)/shard_map/ppermute | solution.py:223
  137.4 5.6 %shard_map.31.refs_0_ = f32[4,2,512,2048]{3,2,1,0:T(8,128)} custom-call(s32[2]{0:T(128)} %pad_add_fusion.5.place_ref, bf16[512,1536]{1,0:T(8,128)(2,1)} %bitcast.4.own_ref.other_ref, bf16[512,1536]{1,0:T(8,128)(2,1)} %bitcast.4.own_ref.other_ref, f32[4,2,512,2048]{3,2,1,0:T(8,128)} %get-tuple-element.25.refs_0_), custom_call_target="tpu_custom_call", output_to_operand_aliasing={{}: (3, {})} | custom-call | flops 1610612736 | bytes 5242880 | tf_op jit(solution)/shard_map/pallas_call | solution.py:95
  143.0 5.4 %shard_map.32._ = f32[4,2,512,2048]{3,2,1,0:T(8,128)} custom-call(s32[2]{0:T(128)} %pad_add_fusion.4.place_ref, bf16[512,1536]{1,0:T(8,128)(2,1)} %bitcast.4.own_ref.other_ref, bf16[512,1536]{1,0:T(8,128)(2,1)} %collective-permute-done.2.other_ref.end_ref, f32[4,2,512,2048]{3,2,1,0:T(8,128)} %shard_map.31.refs_0_), custom_call_target="tpu_custom_call", output_to_operand_aliasing={{}: (3, {})} | custom-call | flops 1610612736 | bytes 5242880 | tf_op jit(solution)/shard_map/pallas_call | solution.py:95
  148.4 4.8 %shard_map.33 = (f32[4,2,512,2048]{3,2,1,0:T(8,128)}, bf16[2,512,512]{2,1,0:T(8,128)(2,1)}) custom-call(s32[2]{0:T(128)} %pad_add_fusion.3.place_ref, bf16[512,1536]{1,0:T(8,128)(2,1)} %bitcast.4.own_ref.other_ref, bf16[512,1536]{1,0:T(8,128)(2,1)} %collective-permute-done.2.other_ref.end_ref, ...), custom_call_target="tpu_custom_call", output_to_operand_aliasing={{0}: (5, {})} | custom-call | flops 3221225472 | bytes 9437184 | tf_op jit(solution)/shard_map/pallas_call | solution.py:129
  153.1 10.5 %collective-permute-done.8.end_ref.other_ref = bf16[512,1536]{1,0:T(8,128)(2,1)} collective-permute-done((bf16[512,1536]{1,0:T(8,128)(2,1)S(1)}, bf16[512,1536]{1,0:T(8,128)(2,1)}, u32[]{:S(2)}, u32[]{:S(2)}) %collective-permute-start.8) | collective-permute-done | bytes 1572896 | tf_op jit(solution)/shard_map/ppermute | solution.py:223
  167.3 4.8 %shard_map.34 = (f32[4,2,512,2048]{3,2,1,0:T(8,128)}, bf16[2,512,512]{2,1,0:T(8,128)(2,1)}) custom-call(s32[2]{0:T(128)} %pad_add_fusion.1.place_ref, bf16[512,1536]{1,0:T(8,128)(2,1)} %bitcast.7.own_ref.other_ref, bf16[512,1536]{1,0:T(8,128)(2,1)} %collective-permute-done.4.other_ref.end_ref, ...), custom_call_target="tpu_custom_call", output_to_operand_aliasing={{0}: (5, {})} | custom-call | flops 3221225472 | bytes 9437184 | tf_op jit(solution)/shard_map/pallas_call | solution.py:129
  172.0 5.5 %shard_map.35._ = f32[4,2,512,2048]{3,2,1,0:T(8,128)} custom-call(s32[2]{0:T(128)} %pad_add_fusion.5.place_ref, bf16[512,1536]{1,0:T(8,128)(2,1)} %bitcast.20, bf16[512,1536]{1,0:T(8,128)(2,1)} %bitcast.21, f32[4,2,512,2048]{3,2,1,0:T(8,128)} %get-tuple-element.28.refs_0_), custom_call_target="tpu_custom_call", output_to_operand_aliasing={{}: (3, {})} | custom-call | flops 1610612736 | bytes 5242880 | tf_op jit(solution)/shard_map/pallas_call | solution.py:95
  177.5 5.2 %shard_map.36 = (f32[4,2,512,2048]{3,2,1,0:T(8,128)}, bf16[2,512,512]{2,1,0:T(8,128)(2,1)}) custom-call(s32[2]{0:T(128)} %pad_add_fusion.4.place_ref, bf16[512,1536]{1,0:T(8,128)(2,1)} %bitcast.22, bf16[512,1536]{1,0:T(8,128)(2,1)} %collective-permute-done.8.end_ref.other_ref, ...), custom_call_target="tpu_custom_call", output_to_operand_aliasing={{0}: (5, {})} | custom-call | flops 3221225472 | bytes 9437184 | tf_op jit(solution)/shard_map/pallas_call | solution.py:129
  184.0 5.2 %shard_map.37 = (f32[4,2,512,2048]{3,2,1,0:T(8,128)}, bf16[2,512,512]{2,1,0:T(8,128)(2,1)}) custom-call(s32[2]{0:T(128)} %pad_add_fusion.3.place_ref, bf16[512,1536]{1,0:T(8,128)(2,1)} %bitcast.24, bf16[512,1536]{1,0:T(8,128)(2,1)} %collective-permute-done.8.end_ref.other_ref, ...), custom_call_target="tpu_custom_call", output_to_operand_aliasing={{0}: (5, {})} | custom-call | flops 3221225472 | bytes 9437184 | tf_op jit(solution)/shard_map/pallas_call | solution.py:129
  189.2 7.5 %collective-permute-done.end_ref.other_ref = bf16[512,1536]{1,0:T(8,128)(2,1)} collective-permute-done((bf16[512,1536]{1,0:T(8,128)(2,1)S(1)}, bf16[512,1536]{1,0:T(8,128)(2,1)}, u32[]{:S(2)}, u32[]{:S(2)}) %collective-permute-start) | collective-permute-done | bytes 1572896 | tf_op jit(solution)/shard_map/ppermute | solution.py:223
  198.8 5.3 %shard_map.38 = (f32[4,2,512,2048]{3,2,1,0:T(8,128)}, bf16[2,512,512]{2,1,0:T(8,128)(2,1)}) custom-call(s32[2]{0:T(128)} %pad_add_fusion.1.place_ref, bf16[512,1536]{1,0:T(8,128)(2,1)} %bitcast.4.own_ref.other_ref, bf16[512,1536]{1,0:T(8,128)(2,1)} %collective-permute-done.2.other_ref.end_ref, ...), custom_call_target="tpu_custom_call", output_to_operand_aliasing={{0}: (5, {})} | custom-call | flops 3221225472 | bytes 9437184 | tf_op jit(solution)/shard_map/pallas_call | solution.py:129
  204.0 5.5 %shard_map.39._ = f32[4,2,512,2048]{3,2,1,0:T(8,128)} custom-call(s32[2]{0:T(128)} %pad_add_fusion.5.place_ref, bf16[512,1536]{1,0:T(8,128)(2,1)} %bitcast.12, bf16[512,1536]{1,0:T(8,128)(2,1)} %bitcast.13, f32[4,2,512,2048]{3,2,1,0:T(8,128)} %get-tuple-element.34.refs_0_), custom_call_target="tpu_custom_call", output_to_operand_aliasing={{}: (3, {})} | custom-call | flops 1610612736 | bytes 5242880 | tf_op jit(solution)/shard_map/pallas_call | solution.py:95
  209.5 5.1 %shard_map.40 = (f32[4,2,512,2048]{3,2,1,0:T(8,128)}, bf16[2,512,512]{2,1,0:T(8,128)(2,1)}) custom-call(s32[2]{0:T(128)} %pad_add_fusion.4.place_ref, bf16[512,1536]{1,0:T(8,128)(2,1)} %bitcast.14, bf16[512,1536]{1,0:T(8,128)(2,1)} %collective-permute-done.end_ref.other_ref, ...), custom_call_target="tpu_custom_call", output_to_operand_aliasing={{0}: (5, {})} | custom-call | flops 3221225472 | bytes 9437184 | tf_op jit(solution)/shard_map/pallas_call | solution.py:129
  217.5 4.8 %shard_map.41 = (f32[4,2,512,2048]{3,2,1,0:T(8,128)}, bf16[2,512,512]{2,1,0:T(8,128)(2,1)}) custom-call(s32[2]{0:T(128)} %pad_add_fusion.3.place_ref, bf16[512,1536]{1,0:T(8,128)(2,1)} %bitcast.16, bf16[512,1536]{1,0:T(8,128)(2,1)} %collective-permute-done.end_ref.other_ref, ...), custom_call_target="tpu_custom_call", output_to_operand_aliasing={{0}: (5, {})} | custom-call | flops 3221225472 | bytes 9437184 | tf_op jit(solution)/shard_map/pallas_call | solution.py:129
  222.3 5.2 %shard_map.42 = (f32[4,2,512,2048]{3,2,1,0:T(8,128)}, bf16[2,512,512]{2,1,0:T(8,128)(2,1)}) custom-call(s32[2]{0:T(128)} %pad_add_fusion.1.place_ref, bf16[512,1536]{1,0:T(8,128)(2,1)} %bitcast.25, bf16[512,1536]{1,0:T(8,128)(2,1)} %collective-permute-done.8.end_ref.other_ref, ...), custom_call_target="tpu_custom_call", output_to_operand_aliasing={{0}: (5, {})} | custom-call | flops 3221225472 | bytes 9437184 | tf_op jit(solution)/shard_map/pallas_call | solution.py:129
  230.5 63.6 %collective-permute-done.13.refs_1_ = bf16[2,512,512]{2,1,0:T(8,128)(2,1)} collective-permute-done((bf16[2,512,512]{2,1,0:T(8,128)(2,1)}, bf16[2,512,512]{2,1,0:T(8,128)(2,1)}, u32[]{:S(2)}, u32[]{:S(2)}) %collective-permute-start.13) | collective-permute-done | bytes 1048608 | tf_op jit(solution)/shard_map/ppermute | solution.py:223
  295.4 4.3 settle.5.refs_2_
  301.0 28.5 %collective-permute-done.11.refs_1_ = bf16[2,512,512]{2,1,0:T(8,128)(2,1)S(1)} collective-permute-done((bf16[2,512,512]{2,1,0:T(8,128)(2,1)}, bf16[2,512,512]{2,1,0:T(8,128)(2,1)S(1)}, u32[]{:S(2)}, u32[]{:S(2)}) %collective-permute-start.11) | collective-permute-done | bytes 1048608 | tf_op jit(solution)/shard_map/ppermute | solution.py:223
  331.8 4.3 settle.6._
  337.5 4.8 %shard_map.43 = (f32[4,2,512,2048]{3,2,1,0:T(8,128)}, bf16[2,512,512]{2,1,0:T(8,128)(2,1)}) custom-call(s32[2]{0:T(128)} %pad_add_fusion.1.place_ref, bf16[512,1536]{1,0:T(8,128)(2,1)} %bitcast.17, bf16[512,1536]{1,0:T(8,128)(2,1)} %collective-permute-done.end_ref.other_ref, bf16[512,1536]{1,0:T(8,128)(2,1)} %copy-done.2, ...), custom_call_target="tpu_custom_call", output_to_operand_aliasing={{0}: (5, {})} | custom-call | flops 3221225472 | bytes 9437184 | tf_op jit(solution)/shard_map/pallas_call | solution.py:129
  342.3 9.8 %collective-permute-done.21.refs_2_ = bf16[2,512,512]{2,1,0:T(8,128)(2,1)} collective-permute-done((bf16[2,512,512]{2,1,0:T(8,128)(2,1)}, bf16[2,512,512]{2,1,0:T(8,128)(2,1)}, u32[]{:S(2)}, u32[]{:S(2)}) %collective-permute-start.21) | collective-permute-done | bytes 1048608 | tf_op jit(solution)/shard_map/ppermute | solution.py:223
  355.3 19.3 %collective-permute-done.20.refs_1_ = bf16[2,512,512]{2,1,0:T(8,128)(2,1)} collective-permute-done((bf16[2,512,512]{2,1,0:T(8,128)(2,1)}, bf16[2,512,512]{2,1,0:T(8,128)(2,1)}, u32[]{:S(2)}, u32[]{:S(2)}) %collective-permute-start.20) | collective-permute-done | bytes 1048608 | tf_op jit(solution)/shard_map/ppermute | solution.py:223
  374.6 22.5 %collective-permute-done.19.refs_0_ = bf16[2,512,512]{2,1,0:T(8,128)(2,1)} collective-permute-done((bf16[2,512,512]{2,1,0:T(8,128)(2,1)}, bf16[2,512,512]{2,1,0:T(8,128)(2,1)}, u32[]{:S(2)}, u32[]{:S(2)}) %collective-permute-start.19) | collective-permute-done | bytes 1048608 | tf_op jit(solution)/shard_map/ppermute | solution.py:223
  397.1 5.3 %settle.7.refs_2_ = f32[4,2,512,2048]{3,2,1,0:T(8,128)} custom-call(s32[4]{0:T(128)} %pad_add_fusion.7.place_ref, bf16[2,512,512]{2,1,0:T(8,128)(2,1)} %collective-permute-done.19.refs_0_, bf16[2,512,512]{2,1,0:T(8,128)(2,1)} %collective-permute-done.20.refs_1_, ...), custom_call_target="tpu_custom_call", output_to_operand_aliasing={{}: (4, {})} | custom-call | flops 1572864 | bytes 9437184 | tf_op jit(solution)/shard_map/settle/pallas_call | solution.py:180
  402.4 17.1 %collective-permute-done.18.refs_1_ = bf16[2,512,512]{2,1,0:T(8,128)(2,1)S(1)} collective-permute-done((bf16[2,512,512]{2,1,0:T(8,128)(2,1)}, bf16[2,512,512]{2,1,0:T(8,128)(2,1)S(1)}, u32[]{:S(2)}, u32[]{:S(2)}) %collective-permute-start.18) | collective-permute-done | bytes 1048608 | tf_op jit(solution)/shard_map/ppermute | solution.py:223
  419.4 22.6 %collective-permute-done.17.refs_0_ = bf16[2,512,512]{2,1,0:T(8,128)(2,1)} collective-permute-done((bf16[2,512,512]{2,1,0:T(8,128)(2,1)}, bf16[2,512,512]{2,1,0:T(8,128)(2,1)}, u32[]{:S(2)}, u32[]{:S(2)}) %collective-permute-start.17) | collective-permute-done | bytes 1048608 | tf_op jit(solution)/shard_map/ppermute | solution.py:223
  442.0 4.3 settle.8.refs_1_
  446.3 16.2 %collective-permute-done.16.refs_0_ = bf16[2,512,512]{2,1,0:T(8,128)(2,1)S(1)} collective-permute-done((bf16[2,512,512]{2,1,0:T(8,128)(2,1)}, bf16[2,512,512]{2,1,0:T(8,128)(2,1)S(1)}, u32[]{:S(2)}, u32[]{:S(2)}) %collective-permute-start.16) | collective-permute-done | bytes 1048608 | tf_op jit(solution)/shard_map/ppermute | solution.py:223
  463.5 3.3 settle.9
  (49 shorter events, 34.7 us)
Async XLA Ops:
  3.8 26.3 %all-to-all-start.2 = ((bf16[8,64,1536]{2,1,0:T(8,128)(2,1)}), bf16[8,64,1536]{2,1,0:T(8,128)(2,1)}, u32[]{:S(2)}, u32[]{:S(2)}) async-start(bf16[8,64,1536]{2,1,0:T(8,128)(2,1)} %equalize.6), calls=%async_computation.2 | async-start | bytes 3145728 | tf_op jit(solution)/shard_map/all_to_all | solution.py:227
  30.2 25.3 %all-to-all-start.1 = ((bf16[8,64,1536]{2,1,0:T(8,128)(2,1)}), bf16[8,64,1536]{2,1,0:T(8,128)(2,1)}, u32[]{:S(2)}, u32[]{:S(2)}) async-start(bf16[8,64,1536]{2,1,0:T(8,128)(2,1)} %equalize.5), calls=%async_computation.1 | async-start | bytes 3145728 | tf_op jit(solution)/shard_map/all_to_all | solution.py:227
  55.5 24.5 %all-to-all-start.3 = ((bf16[8,64,1536]{2,1,0:T(8,128)(2,1)}), bf16[8,64,1536]{2,1,0:T(8,128)(2,1)S(1)}, u32[]{:S(2)}, u32[]{:S(2)}) async-start(bf16[8,64,1536]{2,1,0:T(8,128)(2,1)} %equalize.7), calls=%async_computation.3 | async-start | bytes 3145728 | tf_op jit(solution)/shard_map/all_to_all | solution.py:227
  59.1 37.7 %collective-permute-start.4 = (bf16[512,1536]{1,0:T(8,128)(2,1)}, bf16[512,1536]{1,0:T(8,128)(2,1)}, u32[]{:S(2)}, u32[]{:S(2)}) collective-permute-start(bf16[512,1536]{1,0:T(8,128)(2,1)} %bitcast.7.own_ref.other_ref), channel_id=1, source_target_pairs={{0,1},{3,2},{1,0},{2,3},{4,5},{7,6},{5,4},{6,7},{8,9},{11,10},{9,8... | collective-permute-start | bytes 4718600 | tf_op jit(solution)/shard_map/ppermute | solution.py:223
  61.2 50.6 %collective-permute-start.5 = (bf16[512,1536]{1,0:T(8,128)(2,1)}, bf16[512,1536]{1,0:T(8,128)(2,1)}, u32[]{:S(2)}, u32[]{:S(2)}) collective-permute-start(bf16[512,1536]{1,0:T(8,128)(2,1)} %bitcast.7.own_ref.other_ref), channel_id=1, source_target_pairs={{1,2},{2,1},{5,6},{6,5},{9,10},{10,9},{13,14},{14,13},{17,18},{18,... | collective-permute-start | bytes 4718600 | tf_op jit(solution)/shard_map/ppermute | solution.py:223
  63.0 67.1 %collective-permute-start.2 = (bf16[512,1536]{1,0:T(8,128)(2,1)}, bf16[512,1536]{1,0:T(8,128)(2,1)}, u32[]{:S(2)}, u32[]{:S(2)}) collective-permute-start(bf16[512,1536]{1,0:T(8,128)(2,1)} %bitcast.4.own_ref.other_ref), channel_id=1, source_target_pairs={{0,1},{3,2},{1,0},{2,3},{4,5},{7,6},{5,4},{6,7},{8,9},{11,10},{9,8... | collective-permute-start | bytes 4718600 | tf_op jit(solution)/shard_map/ppermute | solution.py:223
  66.3 69.2 %collective-permute-start.3 = (bf16[512,1536]{1,0:T(8,128)(2,1)}, bf16[512,1536]{1,0:T(8,128)(2,1)}, u32[]{:S(2)}, u32[]{:S(2)}) collective-permute-start(bf16[512,1536]{1,0:T(8,128)(2,1)} %bitcast.4.own_ref.other_ref), channel_id=1, source_target_pairs={{1,2},{2,1},{5,6},{6,5},{9,10},{10,9},{13,14},{14,13},{17,18},{18,... | collective-permute-start | bytes 4718600 | tf_op jit(solution)/shard_map/ppermute | solution.py:223
  80.0 31.8 %copy-start.1 = (bf16[8,64,1536]{2,1,0:T(8,128)(2,1)}, bf16[8,64,1536]{2,1,0:T(8,128)(2,1)S(1)}, u32[]{:S(2)}) copy-start(bf16[8,64,1536]{2,1,0:T(8,128)(2,1)S(1)} %all-to-all-done.3) | copy-start | bytes 4718596
  80.0 38.8 %all-to-all-start = ((bf16[8,64,1536]{2,1,0:T(8,128)(2,1)}), bf16[8,64,1536]{2,1,0:T(8,128)(2,1)S(1)}, u32[]{:S(2)}, u32[]{:S(2)}) async-start(bf16[8,64,1536]{2,1,0:T(8,128)(2,1)} %equalize.4), calls=%async_computation | async-start | bytes 3145728 | tf_op jit(solution)/shard_map/all_to_all | solution.py:227
  83.6 80.0 %collective-permute-start.8 = (bf16[512,1536]{1,0:T(8,128)(2,1)S(1)}, bf16[512,1536]{1,0:T(8,128)(2,1)}, u32[]{:S(2)}, u32[]{:S(2)}) collective-permute-start(bf16[512,1536]{1,0:T(8,128)(2,1)S(1)} %bitcast.18), channel_id=1, source_target_pairs={{0,1},{3,2},{4,5},{7,6},{8,9},{11,10},{12,13},{15,14},{16,17},{19,... | collective-permute-start | bytes 4718600 | tf_op jit(solution)/shard_map/ppermute | solution.py:223
  96.8 68.7 %collective-permute-start.10 = (bf16[512,1536]{1,0:T(8,128)(2,1)}, bf16[512,1536]{1,0:T(8,128)(2,1)}, u32[]{:S(2)}, u32[]{:S(2)}) collective-permute-start(bf16[512,1536]{1,0:T(8,128)(2,1)} %collective-permute-done.4.other_ref.end_ref), channel_id=1, source_target_pairs={{1,2},{2,1},{5,6},{6,5},{9,10},{10,9},{13,14},{14,13},{17,18},{18,... | collective-permute-start | bytes 4718600 | tf_op jit(solution)/shard_map/ppermute | solution.py:223
  111.8 70.8 %collective-permute-start.9 = (bf16[512,1536]{1,0:T(8,128)(2,1)S(1)}, bf16[512,1536]{1,0:T(8,128)(2,1)}, u32[]{:S(2)}, u32[]{:S(2)}) collective-permute-start(bf16[512,1536]{1,0:T(8,128)(2,1)S(1)} %bitcast.19), channel_id=1, source_target_pairs={{1,2},{2,1},{5,6},{6,5},{9,10},{10,9},{13,14},{14,13},{17,18},{18,... | collective-permute-start | bytes 4718600 | tf_op jit(solution)/shard_map/ppermute | solution.py:223
  118.8 44.8 %copy-start = (bf16[8,64,1536]{2,1,0:T(8,128)(2,1)}, bf16[8,64,1536]{2,1,0:T(8,128)(2,1)S(1)}, u32[]{:S(2)}) copy-start(bf16[8,64,1536]{2,1,0:T(8,128)(2,1)S(1)} %all-to-all-done) | copy-start | bytes 4718596
  130.1 66.6 %collective-permute-start = (bf16[512,1536]{1,0:T(8,128)(2,1)S(1)}, bf16[512,1536]{1,0:T(8,128)(2,1)}, u32[]{:S(2)}, u32[]{:S(2)}) collective-permute-start(bf16[512,1536]{1,0:T(8,128)(2,1)S(1)} %bitcast.10), channel_id=1, source_target_pairs={{0,1},{3,2},{4,5},{7,6},{8,9},{11,10},{12,13},{15,14},{16,17},{19,... | collective-permute-start | bytes 4718600 | tf_op jit(solution)/shard_map/ppermute | solution.py:223
  135.6 62.4 %collective-permute-start.7 = (bf16[512,1536]{1,0:T(8,128)(2,1)}, bf16[512,1536]{1,0:T(8,128)(2,1)}, u32[]{:S(2)}, u32[]{:S(2)}) collective-permute-start(bf16[512,1536]{1,0:T(8,128)(2,1)} %collective-permute-done.2.other_ref.end_ref), channel_id=1, source_target_pairs={{1,2},{2,1},{5,6},{6,5},{9,10},{10,9},{13,14},{14,13},{17,18},{18,... | collective-permute-start | bytes 4718600 | tf_op jit(solution)/shard_map/ppermute | solution.py:223
  163.6 51.0 %collective-permute-start.15 = (bf16[512,1536]{1,0:T(8,128)(2,1)S(1)}, bf16[512,1536]{1,0:T(8,128)(2,1)}, u32[]{:S(2)}, u32[]{:S(2)}) collective-permute-start(bf16[512,1536]{1,0:T(8,128)(2,1)S(1)} %bitcast.11), channel_id=1, source_target_pairs={{1,2},{2,1},{5,6},{6,5},{9,10},{10,9},{13,14},{14,13},{17,18},{18,... | collective-permute-start | bytes 4718600 | tf_op jit(solution)/shard_map/ppermute | solution.py:223
  165.4 50.5 %collective-permute-start.14 = (bf16[512,1536]{1,0:T(8,128)(2,1)}, bf16[512,1536]{1,0:T(8,128)(2,1)}, u32[]{:S(2)}, u32[]{:S(2)}) collective-permute-start(bf16[512,1536]{1,0:T(8,128)(2,1)} %collective-permute-done.8.end_ref.other_ref), channel_id=1, source_target_pairs={{1,2},{2,1},{5,6},{6,5},{9,10},{10,9},{13,14},{14,13},{17,18},{18,... | collective-permute-start | bytes 4718600 | tf_op jit(solution)/shard_map/ppermute | solution.py:223
  182.7 45.9 %collective-permute-start.12 = (bf16[2,512,512]{2,1,0:T(8,128)(2,1)}, bf16[2,512,512]{2,1,0:T(8,128)(2,1)}, u32[]{:S(2)}, u32[]{:S(2)}) collective-permute-start(bf16[2,512,512]{2,1,0:T(8,128)(2,1)} %get-tuple-element.32), channel_id=1, source_target_pairs={{1,0},{2,3},{5,4},{6,7},{9,8},{10,11},{13,12},{14,15},{17,16},{18,... | collective-permute-start | bytes 3145736 | tf_op jit(solution)/shard_map/ppermute | solution.py:223
  196.7 103.0 %collective-permute-start.6 = (bf16[2,512,512]{2,1,0:T(8,128)(2,1)}, bf16[2,512,512]{2,1,0:T(8,128)(2,1)}, u32[]{:S(2)}, u32[]{:S(2)}) collective-permute-start(bf16[2,512,512]{2,1,0:T(8,128)(2,1)} %get-tuple-element.26), channel_id=1, source_target_pairs={{1,0},{2,3},{5,4},{6,7},{9,8},{10,11},{13,12},{14,15},{17,16},{18,... | collective-permute-start | bytes 3145736 | tf_op jit(solution)/shard_map/ppermute | solution.py:223
  198.0 138.2 %collective-permute-start.1 = (bf16[512,1536]{1,0:T(8,128)(2,1)}, bf16[512,1536]{1,0:T(8,128)(2,1)S(1)}, u32[]{:S(2)}, u32[]{:S(2)}) collective-permute-start(bf16[512,1536]{1,0:T(8,128)(2,1)} %collective-permute-done.end_ref.other_ref), channel_id=1, source_target_pairs={{1,2},{2,1},{5,6},{6,5},{9,10},{10,9},{13,14},{14,13},{17,18},{18,... | collective-permute-start | bytes 4718600 | tf_op jit(solution)/shard_map/ppermute | solution.py:223
  214.7 79.4 %collective-permute-start.13 = (bf16[2,512,512]{2,1,0:T(8,128)(2,1)}, bf16[2,512,512]{2,1,0:T(8,128)(2,1)}, u32[]{:S(2)}, u32[]{:S(2)}) collective-permute-start(bf16[2,512,512]{2,1,0:T(8,128)(2,1)} %get-tuple-element.33), channel_id=1, source_target_pairs={{1,0},{2,3},{5,4},{6,7},{9,8},{10,11},{13,12},{14,15},{17,16},{18,... | collective-permute-start | bytes 3145736 | tf_op jit(solution)/shard_map/ppermute | solution.py:223
  216.0 113.6 %collective-permute-start.11 = (bf16[2,512,512]{2,1,0:T(8,128)(2,1)}, bf16[2,512,512]{2,1,0:T(8,128)(2,1)S(1)}, u32[]{:S(2)}, u32[]{:S(2)}) collective-permute-start(bf16[2,512,512]{2,1,0:T(8,128)(2,1)} %get-tuple-element.31), channel_id=1, source_target_pairs={{1,0},{2,3},{5,4},{6,7},{9,8},{10,11},{13,12},{14,15},{17,16},{18,... | collective-permute-start | bytes 3145736 | tf_op jit(solution)/shard_map/ppermute | solution.py:223
  228.5 123.6 %collective-permute-start.21 = (bf16[2,512,512]{2,1,0:T(8,128)(2,1)}, bf16[2,512,512]{2,1,0:T(8,128)(2,1)}, u32[]{:S(2)}, u32[]{:S(2)}) collective-permute-start(bf16[2,512,512]{2,1,0:T(8,128)(2,1)} %get-tuple-element.43), channel_id=1, source_target_pairs={{1,0},{2,3},{5,4},{6,7},{9,8},{10,11},{13,12},{14,15},{17,16},{18,... | collective-permute-start | bytes 3145736 | tf_op jit(solution)/shard_map/ppermute | solution.py:223
  294.1 80.5 %collective-permute-start.20 = (bf16[2,512,512]{2,1,0:T(8,128)(2,1)}, bf16[2,512,512]{2,1,0:T(8,128)(2,1)}, u32[]{:S(2)}, u32[]{:S(2)}) collective-permute-start(bf16[2,512,512]{2,1,0:T(8,128)(2,1)} %get-tuple-element.42), channel_id=1, source_target_pairs={{1,0},{2,3},{5,4},{6,7},{9,8},{10,11},{13,12},{14,15},{17,16},{18,... | collective-permute-start | bytes 3145736 | tf_op jit(solution)/shard_map/ppermute | solution.py:223
  299.7 97.3 %collective-permute-start.19 = (bf16[2,512,512]{2,1,0:T(8,128)(2,1)}, bf16[2,512,512]{2,1,0:T(8,128)(2,1)}, u32[]{:S(2)}, u32[]{:S(2)}) collective-permute-start(bf16[2,512,512]{2,1,0:T(8,128)(2,1)} %get-tuple-element.41), channel_id=1, source_target_pairs={{1,0},{2,3},{5,4},{6,7},{9,8},{10,11},{13,12},{14,15},{17,16},{18,... | collective-permute-start | bytes 3145736 | tf_op jit(solution)/shard_map/ppermute | solution.py:223
  329.5 1.0 copy-start.4
  330.6 88.9 %collective-permute-start.18 = (bf16[2,512,512]{2,1,0:T(8,128)(2,1)}, bf16[2,512,512]{2,1,0:T(8,128)(2,1)S(1)}, u32[]{:S(2)}, u32[]{:S(2)}) collective-permute-start(bf16[2,512,512]{2,1,0:T(8,128)(2,1)} %get-tuple-element.40), channel_id=1, source_target_pairs={{1,0},{2,3},{5,4},{6,7},{9,8},{10,11},{13,12},{14,15},{17,16},{18,... | collective-permute-start | bytes 3145736 | tf_op jit(solution)/shard_map/ppermute | solution.py:223
  336.2 1.3 copy-start.2
  336.2 105.8 %collective-permute-start.17 = (bf16[2,512,512]{2,1,0:T(8,128)(2,1)}, bf16[2,512,512]{2,1,0:T(8,128)(2,1)}, u32[]{:S(2)}, u32[]{:S(2)}) collective-permute-start(bf16[2,512,512]{2,1,0:T(8,128)(2,1)} %get-tuple-element.39), channel_id=1, source_target_pairs={{1,0},{2,3},{5,4},{6,7},{9,8},{10,11},{13,12},{14,15},{17,16},{18,... | collective-permute-start | bytes 3145736 | tf_op jit(solution)/shard_map/ppermute | solution.py:223
  352.1 110.4 %collective-permute-start.16 = (bf16[2,512,512]{2,1,0:T(8,128)(2,1)}, bf16[2,512,512]{2,1,0:T(8,128)(2,1)S(1)}, u32[]{:S(2)}, u32[]{:S(2)}) collective-permute-start(bf16[2,512,512]{2,1,0:T(8,128)(2,1)} %get-tuple-element.38), channel_id=1, source_target_pairs={{1,0},{2,3},{5,4},{6,7},{9,8},{10,11},{13,12},{14,15},{17,16},{18,... | collective-permute-start | bytes 3145736 | tf_op jit(solution)/shard_map/ppermute | solution.py:223
  419.4 22.6 %copy-start.3 = (bf16[2,512,512]{2,1,0:T(8,128)(2,1)}, bf16[2,512,512]{2,1,0:T(8,128)(2,1)S(1)}, u32[]{:S(2)}) copy-start(bf16[2,512,512]{2,1,0:T(8,128)(2,1)S(1)} %collective-permute-done.18.refs_1_) | copy-start | bytes 3145732
  462.5 1.0 copy-start.5
